TPU v7x, 128 devices: a whole 4x4x4 slice. The times are simulated.
128 devices in a mesh: row: 16 (over y, z), col: 8 (over x, core).
Axes of the slice: x: 4, y: 4, z: 4, core: 2. Of those that a mesh axis runs over, the one named last changes fastest.
Arguments:
- eigvec_halves: float32 [3072, 32768], P('col', 'row'), may hold values from -6 to 6
- rotation_mate: int32 [3072], replicated, may hold values from 0 to 3071, as said below
- givens_theta: float32 [3072], replicated, may hold values from -3.140625 to 3.140625
- kept_vectors: int32 [3072], replicated, may hold values from 0 to 3071, as said below
- secular_singularities: float32 [3072], replicated, may hold values from -0.25 to 3071.25, as said below
- secular_coefficients: float32 [3072], replicated, may hold values from -6 to 6
- secular_zeros: float32 [512], replicated, may hold values from 0.4 to 3071.6
Outputs:
- packed_vectors: float32 [3072, 32768], P(('row', 'col'))
- panel: float32 [512, 32768], P('col', 'row')
Inputs may be any that keep to these rules, and one draw needn't show every extreme that they name: `rotation_mate`: partner is an involution. Column blocks of 384 belong to the indices of col in order; at most 24 columns of one block pair with columns of any one other block, exactly that many for some two blocks in every draw. `kept_vectors`: survivors is a permutation. Compacted positions form consecutive blocks of 24, one block per device of row+col in order; one block takes at most 4 columns from any one column block of 384, exactly that many from some. secular_singularities[k] lies within 0.25 of k.
All inputs are finite; a program needn't handle non-finite values.
Results may differ from a plain program's by a relative error of at most 0.00007.
Values sent between devices are 32-bit elements; how exact they have to be, the bound alone decides.
No kernel may reach another device: no remote copies, remote signals or barrier semaphores. Data moves between devices by JAX's collectives and lax.ppermute only.
A program may use at most 64 MiB of HBM per device.

v0:
```python
import jax
import jax.numpy as jnp
from jax import lax
from jax.sharding import PartitionSpec as P


def rank_within(groups, member, group_count):
    onehot = (
        (groups[:, None] == jnp.arange(group_count, dtype=jnp.int32)[None, :]) & member[:, None]
    ).astype(jnp.int32)
    before = jnp.cumsum(onehot, axis=0) - onehot
    return jnp.sum(before * onehot, axis=1)


def bucket_table(sort_keys, boundary_keys, capacity):
    ordering = jnp.argsort(sort_keys, stable=True)
    sorted_keys = sort_keys[ordering]
    edge_ids = jnp.searchsorted(sorted_keys, boundary_keys)
    slot_ids = jnp.arange(capacity, dtype=jnp.int32)
    usable = slot_ids[None, :] < (edge_ids[1:] - edge_ids[:-1])[:, None]
    picked = jnp.where(usable, edge_ids[:-1, None] + slot_ids[None, :], 0)
    return (ordering[picked], usable)


def selector(index_list, valid, source_count):
    sources = jnp.arange(source_count, dtype=jnp.int32)[None, :]
    return ((index_list[:, None] == sources) & valid[:, None]).astype(jnp.float32)


def select_rows(index_list, valid, source):
    pick = selector(index_list, valid, source.shape[0])
    return jnp.dot(
        pick, source, precision=lax.Precision.HIGHEST, preferred_element_type=jnp.float32
    )


def shards(
    eigvec_halves,
    rotation_mate,
    givens_theta,
    kept_vectors,
    secular_singularities,
    secular_coefficients,
    secular_zeros,
):
    col_count = lax.axis_size("col")
    row_count = lax.axis_size("row")
    block_cols, block_rows = eigvec_halves.shape
    total_cols = rotation_mate.shape[0]
    panel_cols = secular_zeros.shape[0]
    pair_cap = block_cols // 16
    col_index = lax.axis_index("col")
    first_col = col_index * block_cols
    local_labels = first_col + jnp.arange(block_cols, dtype=jnp.int32)
    mate_ids = lax.dynamic_slice_in_dim(rotation_mate, first_col, block_cols)
    paired = mate_ids != local_labels
    owner_col = mate_ids // block_cols
    remote = paired & (owner_col != col_index)
    pair_keys = jnp.where(remote, owner_col * total_cols + mate_ids, col_count * total_cols)
    pair_edges = jnp.arange(col_count + 1, dtype=jnp.int32) * total_cols
    chosen, usable = bucket_table(pair_keys, pair_edges, pair_cap)
    outgoing = select_rows(chosen.reshape(-1), usable.reshape(-1), eigvec_halves).reshape(
        col_count, pair_cap, block_rows
    )
    incoming = lax.all_to_all(outgoing, "col", split_axis=0, concat_axis=0, tiled=True)
    rank_here = rank_within(owner_col, remote, col_count)
    flat_in = incoming.reshape(col_count * pair_cap, block_rows)
    from_remote = select_rows(owner_col * pair_cap + rank_here, remote, flat_in)
    from_local = select_rows(mate_ids - first_col, paired & jnp.logical_not(remote), eigvec_halves)
    mate_rows = from_remote + from_local
    angles_here = givens_theta[jnp.minimum(local_labels, mate_ids)]
    sign_flip = jnp.where(local_labels < mate_ids, -1.0, 1.0).astype(jnp.float32)
    cosine = jnp.where(paired, jnp.cos(angles_here), 1.0)
    sine_term = jnp.where(paired, sign_flip * jnp.sin(angles_here), 0.0)
    spun_vectors = cosine[:, None] * eigvec_halves + sine_term[:, None] * mate_rows
    spot_sequence = jnp.argsort(kept_vectors)[local_labels]
    cauchy_raw = secular_coefficients[spot_sequence][:, None] / (
        secular_singularities[spot_sequence][:, None] - secular_zeros[None, :]
    )

    def add_block(block_index, running):
        pole_block = lax.dynamic_slice_in_dim(
            secular_singularities, block_index * block_cols, block_cols
        )
        weight_block = lax.dynamic_slice_in_dim(
            secular_coefficients, block_index * block_cols, block_cols
        )
        block_raw = weight_block[:, None] / (pole_block[:, None] - secular_zeros[None, :])
        return running + jnp.sum(block_raw * block_raw, axis=0)

    col_sq = lax.fori_loop(0, col_count, add_block, jnp.zeros((panel_cols,), jnp.float32))
    cauchy = cauchy_raw * lax.rsqrt(col_sq + 1e-06)[None, :]
    panel = lax.psum_scatter(
        lax.dot_general(
            cauchy,
            spun_vectors,
            (((0,), (0,)), ((), ())),
            precision=lax.Precision.HIGHEST,
            preferred_element_type=jnp.float32,
        ),
        "col",
        scatter_dimension=0,
        tiled=True,
    )
    dest_count = row_count * col_count
    every_destination = block_cols // row_count
    share_base = every_destination // col_count
    move_cap = share_base + share_base // 3
    move_edges = jnp.arange(dest_count + 1, dtype=jnp.int32) * every_destination
    chosen_move, usable_move = bucket_table(spot_sequence, move_edges, move_cap)
    parcels = select_rows(chosen_move.reshape(-1), usable_move.reshape(-1), spun_vectors).reshape(
        dest_count, move_cap, block_rows
    )
    arrived = lax.all_to_all(parcels, ("row", "col"), split_axis=0, concat_axis=0, tiled=True)
    arrived = arrived.reshape(row_count, col_count * move_cap, block_rows)
    destination_slot = lax.axis_index("row") * col_count + col_index
    wanted_vectors = lax.dynamic_slice_in_dim(
        kept_vectors, destination_slot * every_destination, every_destination
    )
    source_col = wanted_vectors // block_cols
    source_rank = rank_within(source_col, jnp.ones(source_col.shape, dtype=jnp.bool_), col_count)
    final_pick = selector(
        source_col * move_cap + source_rank,
        jnp.ones(source_col.shape, dtype=jnp.bool_),
        col_count * move_cap,
    )
    placed = lax.dot_general(
        final_pick,
        arrived,
        (((1,), (1,)), ((), ())),
        precision=lax.Precision.HIGHEST,
        preferred_element_type=jnp.float32,
    )
    packed_vectors = placed.reshape(every_destination, row_count * block_rows)
    return (packed_vectors, panel)


def solution(mesh):
    placed = (P("col", "row"), P(), P(), P(), P(), P(), P())
    return jax.shard_map(
        shards,
        mesh=mesh,
        in_specs=placed,
        out_specs=(P(("row", "col"), None), P("col", "row")),
        check_vma=False,
    )
```

profile of v0, /device:TPU:1, one launch (start us, length us, event | category | flops | bytes accessed | tf_op | source)
XLA Modules:
  0.0 192.2 jit_solution(4978052794850783314)
XLA Ops:
  7.2 0.8 compare_select_fusion.5
  8.0 2.5 %gather_fusion.5 = f32[384]{0:T(512)S(1)} fusion(f32[3072]{0:T(1024)S(1)} %copy-done, s32[1024]{0:T(1024)S(1)} %pad_clamp_fusion.5), kind=kCustom, calls=%fused_computation.5 | custom fusion | bytes 4608 | tf_op jit(solution)/shard_map/gather | solution.py:71
  10.5 0.8 cosine_select_fusion
  11.3 0.8 add_select_fusion.1
  12.1 3.8 %sort.50 = (s32[384]{0:T(512)}, s32[384]{0:T(512)S(1)}) sort(s32[384]{0:T(512)S(1)} %get-tuple-element.315, s32[384]{0:T(512)S(1)} %iota.74), dimensions={0}, to_apply=%region_9.10 | sort | flops 3456 | bytes 6144 | tf_op jit(solution)/shard_map/jit(argsort)/sort | solution.py:16
  15.9 2.8 %gather_fusion.6 = s32[384]{0:T(512)S(1)} fusion(s32[384]{0:T(512)S(1)} %get-tuple-element.315, s32[1024]{0:T(1024)S(1)} %pad_clamp_fusion.4), kind=kCustom, calls=%fused_computation.6 | custom fusion | bytes 4608 | tf_op jit(solution)/shard_map/gather | solution.py:17
  18.7 6.5 %while.63 = (s32[]{:T(128)}, u32[9]{0:T(128)S(1)}, u32[9]{0:T(128)S(1)}, s32[384]{0:T(512)S(1)}, s32[]{:T(128)}, /*index=5*/s32[]{:T(128)}, s32[]{}) while((s32[]{:T(128)}, u32[9]{0:T(128)S(1)}, u32[9]{0:T(128)S(1)}, s32[384]{0:T(512)S(1)}, s32[]{:T(128)}, /*index=5*/s32[]{:T(128)}, s32[]{}) %tuple.98), condition=%wide.region_11.12_spmd.clone, body=%wide.region_10.11_spmd.clone.sunk | while | flops 1154 | bytes 4628 | solution.py:18
  18.8 0.7 gather_fusion.1
  19.5 0.7 gather_fusion.1
  20.2 0.7 gather_fusion.1
  20.9 0.7 gather_fusion.1
  21.7 0.7 gather_fusion.1
  22.4 0.7 gather_fusion.1
  23.1 0.7 gather_fusion.1
  25.6 1.6 gather_fusion.7
  27.3 2.9 %fusion.29 = f32[192,2048]{1,0:T(8,128)} fusion(f32[384,2048]{1,0:T(8,128)S(1)} %copy-done.3, s32[192]{0:T(256)S(1)} %gather_fusion.7, pred[192]{0:T(512)(128)(4,1)S(1)} %lt.178), kind=kOutput, calls=%fused_computation.51 | convolution fusion | flops 1812086784 | bytes 4719552 | tf_op jit(solution)/shard_map/dot_general | solution.py:32
  30.2 5.9 %all-to-all-start = ((f32[8,24,2048]{2,1,0:T(8,128)}), f32[8,24,2048]{2,1,0:T(8,128)}, u32[]{:S(2)}, u32[]{:S(2)}) async-start(f32[8,24,2048]{2,1,0:T(8,128)} %bitcast.28), calls=%async_computation | async-start | bytes 3145728 | tf_op jit(solution)/shard_map/all_to_all | solution.py:65
  36.2 5.8 %sort.48 = (s32[3072]{0:T(1024)}, s32[3072]{0:T(1024)S(1)}) sort(s32[3072]{0:T(1024)S(1)} %copy-done.7, s32[3072]{0:T(1024)S(1)} %iota.69), dimensions={0}, to_apply=%region_2.3 | sort | flops 36864 | bytes 49152 | tf_op jit(solution)/shard_map/jit(argsort)/sort | solution.py:76
  41.9 2.5 %gather_fusion.2 = s32[384]{0:T(512)S(1)} fusion(s32[3072]{0:T(1024)S(1)} %get-tuple-element.229, s32[1024]{0:T(1024)S(1)} %pad_clamp_fusion.8), kind=kCustom, calls=%fused_computation.2 | custom fusion | bytes 4608 | tf_op jit(solution)/shard_map/gather | solution.py:76
  44.5 2.5 %gather_fusion.9 = f32[384]{0:T(512)S(1)} fusion(f32[3072]{0:T(1024)S(1)} %copy-done.2, s32[1024]{0:T(1024)S(1)} %pad_clamp_fusion.2), kind=kCustom, calls=%fused_computation.9 | custom fusion | bytes 4608 | tf_op jit(solution)/shard_map/gather | solution.py:78
  47.1 2.5 %gather_fusion.8 = f32[384]{0:T(512)S(1)} fusion(f32[3072]{0:T(1024)S(1)} %copy-done.1, s32[1024]{0:T(1024)S(1)} %pad_clamp_fusion.2), kind=kCustom, calls=%fused_computation.8 | custom fusion | bytes 4608 | tf_op jit(solution)/shard_map/gather | solution.py:77
  49.6 3.3 %while.64 = (s32[]{:T(128)}, f32[512]{0:T(512)S(1)}, f32[3072]{0:T(1024)S(1)}, f32[3072]{0:T(1024)S(1)}, f32[512]{0:T(512)S(1)}, /*index=5*/s32[]{:T(128)}, s32[]{:T(128)}, s32[]{:T(128)}, s32[]{:T(128)}) while((s32[]{:T(128)}, f32[512]{0:T(512)S(1)}, f32[3072]{0:T(1024)S(1)}, f32[3072]{0:T(1024)S(1)}, f32[512]{0:T(512)S(1)}, ...), condition=%wide.region_14.15_spmd.clone, body=%wide.region_12.14_spmd.clone.sunk | while | flops 786951 | bytes 19621 | solution.py:91
  52.9 0.9 reduce-window.6
  54.1 3.8 %sort.49 = (s32[384]{0:T(512)}, s32[384]{0:T(512)S(1)}) sort(s32[384]{0:T(512)S(1)} %gather_fusion.2, s32[384]{0:T(512)S(1)} %iota.71), dimensions={0}, to_apply=%region_3.4 | sort | flops 3456 | bytes 6144 | tf_op jit(solution)/shard_map/jit(argsort)/sort | solution.py:16
  57.8 2.8 %gather_fusion.3 = s32[384]{0:T(512)S(1)} fusion(s32[384]{0:T(512)S(1)} %gather_fusion.2, s32[1024]{0:T(1024)S(1)} %pad_clamp_fusion.7), kind=kCustom, calls=%fused_computation.3 | custom fusion | bytes 4608 | tf_op jit(solution)/shard_map/gather | solution.py:17
  60.8 0.8 multiply_select_fusion
  61.5 4.5 %fusion.16 = f32[384,2048]{1,0:T(8,128)} fusion(f32[384,2048]{1,0:T(8,128)S(1)} %copy-done.3, s32[384]{0:T(512)S(1)} %get-tuple-element.322, pred[384]{0:T(512)(128)(4,1)S(1)} %not_and_fusion), kind=kOutput, calls=%fused_computation.38 | convolution fusion | flops 3624173568 | bytes 6293376 | tf_op jit(solution)/shard_map/dot_general | solution.py:32
  66.0 4.4 %multiply_add_fusion = f32[384,2048]{1,0:T(8,128)S(1)} fusion(f32[384,2048]{1,0:T(8,128)} %fusion.16, f32[384,2048]{1,0:T(8,128)S(1)} %copy-done.3, f32[192,2048]{1,0:T(8,128)} %bitcast.5, f32[384]{0:T(512)S(1)} %multiply_select_fusion, f32[384]{0:T(512)S(1)} %get-tuple-element.313, s32[384]{0:T(512)S(1)} %multiply_add_fusion.1, ...), kind=kOutput, calls=%fused_computation.28 | convolution fusion | flops 1815232512 | bytes 11015040 | tf_op jit(solution)/shard_map/dot_general | solution.py:32
  70.5 1.7 copy-done.4
  72.1 8.5 %fusion.8 = f32[512,2048]{1,0:T(8,128)} fusion(f32[384,2048]{1,0:T(8,128)S(1)} %multiply_add_fusion, f32[512]{0:T(512)S(1)} %add_rsqrt_fusion, f32[512]{0:T(512)S(1)} %get-tuple-element.492, f32[384]{0:T(512)S(1)} %gather_fusion.9, f32[384]{0:T(512)S(1)} %gather_fusion.8), kind=kOutput, calls=%fused_computation.29 | convolution fusion | flops 4832428032 | bytes 7347200 | tf_op jit(solution)/shard_map/dot_general | solution.py:94
  80.7 15.1 %while.62 = (s32[]{:T(128)}, u32[129]{0:T(256)S(1)}, u32[129]{0:T(256)S(1)}, s32[384]{0:T(512)S(1)}, s32[]{:T(128)}, /*index=5*/s32[]{:T(128)}, s32[]{}) while((s32[]{:T(128)}, u32[129]{0:T(256)S(1)}, u32[129]{0:T(256)S(1)}, s32[384]{0:T(512)S(1)}, s32[]{:T(128)}, /*index=5*/s32[]{:T(128)}, s32[]{}) %tuple.101), condition=%wide.region_5.6_spmd.clone, body=%wide.region_4.5_spmd.clone.sunk | while | flops 2834 | bytes 10388 | solution.py:18
  80.7 1.6 gather_fusion
  82.4 1.6 gather_fusion
  84.1 1.6 gather_fusion
  85.8 1.6 gather_fusion
  87.4 1.6 gather_fusion
  89.1 1.6 gather_fusion
  90.8 1.6 gather_fusion
  92.5 1.6 gather_fusion
  94.2 1.6 gather_fusion
  96.3 3.5 %gather_fusion.4 = s32[512]{0:T(512)S(1)} fusion(s32[384]{0:T(512)S(1)} %get-tuple-element.230, s32[1024]{0:T(1024)S(1)} %pad_clamp_fusion.6), kind=kCustom, calls=%fused_computation.4 | custom fusion | bytes 6144 | tf_op jit(solution)/shard_map/gather | solution.py:22
  99.8 5.4 %fusion.13 = f32[512,2048]{1,0:T(8,128)} fusion(f32[384,2048]{1,0:T(8,128)S(1)} %copy-done.5, s32[512]{0:T(512)S(1)} %gather_fusion.4, pred[512]{0:T(512)(128)(4,1)S(1)} %lt.165), kind=kOutput, calls=%fused_computation.35 | convolution fusion | flops 4832231424 | bytes 7342592 | tf_op jit(solution)/shard_map/dot_general | solution.py:32
  105.3 5.2 %reshape.263 = f32[128,4,2048]{2,1,0:T(4,128)} reshape(f32[512,2048]{1,0:T(8,128)} %fusion.13) | data formatting | bytes 8388608 | tf_op jit(solution)/shard_map/reshape | solution.py:111
  110.5 11.0 %all-to-all-start.1 = ((f32[128,4,2048]{2,1,0:T(4,128)}), f32[128,4,2048]{2,1,0:T(4,128)}, u32[]{:S(2)}, u32[]{:S(2)}) async-start(f32[128,4,2048]{2,1,0:T(4,128)} %reshape.263), calls=%async_computation.1 | async-start | bytes 8388608 | tf_op jit(solution)/shard_map/all_to_all | solution.py:114
  122.0 52.1 %all-to-all-done.1 = f32[128,4,2048]{2,1,0:T(4,128)} async-done(((f32[128,4,2048]{2,1,0:T(4,128)}), f32[128,4,2048]{2,1,0:T(4,128)}, u32[]{:S(2)}, u32[]{:S(2)}) %all-to-all-start.1) | async-done | bytes 4194336 | tf_op jit(solution)/shard_map/all_to_all | solution.py:114
  174.1 5.3 %reshape.264 = f32[16,32,2048]{2,1,0:T(8,128)} reshape(f32[128,4,2048]{2,1,0:T(4,128)} %all-to-all-done.1) | data formatting | bytes 8388608 | tf_op jit(solution)/shard_map/reshape | solution.py:115
  179.3 2.5 %copy.11 = f32[16,4,8,2048]{3,2,0,1:T(8,128)S(1)} copy(f32[16,4,8,2048]{3,2,1,0:T(8,128)} %bitcast.27) | data formatting | bytes 8388608 | tf_op jit(solution)/shard_map/dot_general | solution.py:127
  181.8 3.6 %fusion.38 = f32[24,32768]{1,0:T(8,128)} fusion(f32[32768,32]{0,1:T(8,128)S(1)} %bitcast.26, s32[24]{0:T(128)S(1)} %multiply_add_fusion.2), kind=kOutput, calls=%fused_computation.69 | convolution fusion | flops 301990656 | bytes 7340128 | tf_op jit(solution)/shard_map/dot_general | solution.py:127
  (150 shorter events, 6.8 us)
Async XLA Ops:
  7.2 0.8 copy-start
  18.7 8.6 %copy-start.3 = (f32[384,2048]{1,0:T(8,128)S(1)}, f32[384,2048]{1,0:T(8,128)}, u32[]{:S(2)}) copy-start(f32[384,2048]{1,0:T(8,128)} %param.13) | copy-start | bytes 9437188
  27.3 8.9 %copy-start.7 = (s32[3072]{0:T(1024)S(1)}, s32[3072]{0:T(1024)}, u32[]{:S(2)}) copy-start(s32[3072]{0:T(1024)} %param.16) | copy-start | bytes 36868
  30.2 14.3 %copy-start.2 = (f32[3072]{0:T(1024)S(1)}, f32[3072]{0:T(1024)}, u32[]{:S(2)}) copy-start(f32[3072]{0:T(1024)} %param.17) | copy-start | bytes 36868
  30.2 16.9 %copy-start.1 = (f32[3072]{0:T(1024)S(1)}, f32[3072]{0:T(1024)}, u32[]{:S(2)}) copy-start(f32[3072]{0:T(1024)} %param.18) | copy-start | bytes 36868
  30.2 35.8 %all-to-all-start = ((f32[8,24,2048]{2,1,0:T(8,128)}), f32[8,24,2048]{2,1,0:T(8,128)}, u32[]{:S(2)}, u32[]{:S(2)}) async-start(f32[8,24,2048]{2,1,0:T(8,128)} %bitcast.28), calls=%async_computation | async-start | bytes 3145728 | tf_op jit(solution)/shard_map/all_to_all | solution.py:65
  36.1 149.3 %reduce-scatter.2.cloned.1.call-start = ((), (), s32[]{:S(2)}) async-start(), calls=%async_computation.3 | async-start | bytes 4718592 | tf_op jit(solution)/shard_map/reduce_scatter | solution.py:93
  41.9 7.7 %copy-start.6 = (f32[512]{0:T(512)S(1)}, f32[512]{0:T(512)}, u32[]{:S(2)}) copy-start(f32[512]{0:T(512)} %param.19) | copy-start | bytes 6148
  70.4 1.7 copy-start.4
  96.3 3.5 %copy-start.5 = (f32[384,2048]{1,0:T(8,128)S(1)}, f32[384,2048]{1,0:T(8,128)}, u32[]{:S(2)}) copy-start(f32[384,2048]{1,0:T(8,128)} %copy-done.4) | copy-start | bytes 9437188
  110.5 63.6 %all-to-all-start.1 = ((f32[128,4,2048]{2,1,0:T(4,128)}), f32[128,4,2048]{2,1,0:T(4,128)}, u32[]{:S(2)}, u32[]{:S(2)}) async-start(f32[128,4,2048]{2,1,0:T(4,128)} %reshape.263), calls=%async_computation.1 | async-start | bytes 8388608 | tf_op jit(solution)/shard_map/all_to_all | solution.py:114
Sparse Core Ops, SparseCore 0:
  80.8 37.2 reduce-scatter.1
where the time goes:
time: 193 us; the launch traced here: 192 us
  local copies, waits for them, and re-layouts  57.8 us (30%)
  waiting for transfers between devices  52.1 us (27%)
  matrix products  29.3 us (15%)
  other arithmetic  20.9 us (11%)
  starting transfers between devices  16.9 us (9%)
  between operations  14.4 us (7%)
    all_to_all x1, waiting for transfers between devices, shards(): lax.all_to_all(parcels, ('row', 'col'), split_axis=0, concat_axis=0, tile...  52.1 us
    gather x18, local copies, waits for them, and re-layouts, bucket_table(): edge_ids = jnp.searchsorted(sorted_keys, boundary_keys)  20.5 us
    dot_general x4, matrix products, select_rows(): jnp.dot(pick, source, precision=lax.Precision.HIGHEST, preferred_element_...  17.2 us
    all_to_all x1, starting transfers between devices, shards(): lax.all_to_all(parcels, ('row', 'col'), split_axis=0, concat_axis=0, tile...  11 us
    dot_general x1, matrix products, shards(): lax.dot_general(cauchy, spun_vectors, (((0,), (0,)), ((), ())), precision...  8.53 us
    sort x2, other arithmetic, bucket_table(): ordering = jnp.argsort(sort_keys, stable=True)  7.55 us
    all_to_all x1, starting transfers between devices, shards(): lax.all_to_all(outgoing, 'col', split_axis=0, concat_axis=0, tiled=True)  5.92 us
    sort x1, other arithmetic, shards(): spot_sequence = jnp.argsort(kept_vectors)[local_labels]  5.76 us
  transfers between devices with their start and end apart: 3, of which 1 were waited for; matrix products, arithmetic and copies ran while one was open for 37% of the time, Pallas kernels for 0%

commit v1 on v0

v1 whole, which is shorter than its diff:
```python
import functools

import jax
import jax.numpy as jnp
from jax import lax
from jax.experimental import pallas as pl
from jax.experimental.pallas import tpu as pltpu
from jax.sharding import PartitionSpec as P

LANES = 128
SUB = 8


def to_tiles(rows):
    count, width = rows.shape
    tiles = rows.reshape(count // SUB, SUB, width // LANES, LANES)
    return tiles.transpose(0, 2, 1, 3).reshape(count * width // LANES, LANES)


def from_tiles(tiles, count, width):
    rows = tiles.reshape(count // SUB, width // LANES, SUB, LANES)
    return rows.transpose(0, 2, 1, 3).reshape(count, width)


def pack_kernel(lane_tiles, local_rows, mate_ref, dest_ref, cos_ref, sin_ref,
                local_hbm, mates_hbm, out_ref, rows_ref, sems):
    split = local_rows * lane_tiles
    copies = [
        pltpu.make_async_copy(local_hbm, rows_ref.at[pl.ds(0, split)], sems.at[0]),
        pltpu.make_async_copy(
            mates_hbm, rows_ref.at[pl.ds(split, mates_hbm.shape[0])], sems.at[1]
        ),
    ]
    for copy in copies:
        copy.start()
    for copy in copies:
        copy.wait()
    tile_rows = lane_tiles * SUB

    def column(i, carry):
        own = (i // SUB) * tile_rows + i % SUB
        mate = mate_ref[i]
        dest = pl.multiple_of(dest_ref[i], SUB)
        cosine = cos_ref[i]
        sine = sin_ref[i]
        for part in range(lane_tiles // SUB):
            offset = part * SUB * SUB
            a = rows_ref[pl.ds(own + offset, SUB, SUB), :]
            b = rows_ref[pl.ds(mate + offset, SUB, SUB), :]
            out_ref[pl.ds(dest + part * SUB, SUB), :] = cosine * a + sine * b
        return carry

    lax.fori_loop(0, local_rows, column, 0, unroll=4)


def unpack_kernel(lane_tiles, sources, wanted, per_step, start_ref, in_ref, out_ref):
    slots = in_ref.shape[0] // per_step
    for k in range(wanted):
        start = pl.multiple_of(start_ref[k], SUB)
        for r in range(per_step):
            for part in range(lane_tiles // SUB):
                value = in_ref[pl.ds(start + r * slots + part * SUB, SUB), :]
                first = (r * lane_tiles + part * SUB) * SUB + k % SUB
                out_ref[k // SUB, pl.ds(first, SUB, SUB), :] = value


def one_hot_sum(match, values):
    return jnp.sum(jnp.where(match, values[None, :], jnp.zeros((), values.dtype)), axis=1)


def shards(
    eigvec_halves,
    rotation_mate,
    givens_theta,
    kept_vectors,
    secular_singularities,
    secular_coefficients,
    secular_zeros,
):
    col_count = lax.axis_size("col")
    row_count = lax.axis_size("row")
    chips = col_count // 2
    block_cols, block_rows = eigvec_halves.shape
    total_cols = rotation_mate.shape[0]
    panel_cols = secular_zeros.shape[0]
    pair_cap = block_cols // 16
    lane_tiles = block_rows // LANES
    dest_count = row_count * col_count
    every = total_cols // dest_count
    move_cap = every // col_count + every // col_count // 3
    col_index = lax.axis_index("col")
    chip, core = col_index // 2, col_index % 2
    first_col = col_index * block_cols

    order = jnp.arange(block_cols, dtype=jnp.int32)
    labels = first_col + order
    mates = lax.dynamic_slice_in_dim(rotation_mate, first_col, block_cols)
    owner = mates // block_cols
    same_owner = owner[:, None] == owner[None, :]
    send_rank = jnp.sum((same_owner & (order[None, :] < order[:, None])).astype(jnp.int32), axis=1)
    send_slot = jnp.where(owner != col_index, owner * pair_cap + send_rank, -1)
    slots = jnp.arange(col_count * pair_cap, dtype=jnp.int32)
    pick = (slots[:, None] == send_slot[None, :]).astype(jnp.float32)
    outgoing = jnp.dot(
        pick, eigvec_halves, precision=lax.Precision.HIGHEST, preferred_element_type=jnp.float32
    ).reshape(col_count, pair_cap, block_rows)
    incoming = lax.all_to_all(outgoing, "col", split_axis=0, concat_axis=0, tiled=True)
    flat_in = incoming.reshape(col_count * pair_cap, block_rows)

    paired = mates != labels
    own_match = kept_vectors[None, :] == labels[:, None]
    mate_match = kept_vectors[None, :] == mates[:, None]
    positions = jnp.arange(total_cols, dtype=jnp.int32)
    spot = one_hot_sum(own_match, positions)
    pole = one_hot_sum(own_match, secular_singularities)
    weight = one_hot_sum(own_match, secular_coefficients)
    mate_pole = one_hot_sum(mate_match, secular_singularities)
    mate_weight = one_hot_sum(mate_match, secular_coefficients)
    angle = one_hot_sum(positions[None, :] == jnp.minimum(labels, mates)[:, None], givens_theta)
    sign_flip = jnp.where(labels < mates, -1.0, 1.0).astype(jnp.float32)
    cosine = jnp.where(paired, jnp.cos(angle), 1.0)
    sine = jnp.where(paired, sign_flip * jnp.sin(angle), 0.0)

    recv_rank = jnp.sum((same_owner & (mates[None, :] < mates[:, None])).astype(jnp.int32), axis=1)
    mate_row = jnp.where(
        owner != col_index, block_cols + owner * pair_cap + recv_rank, mates - first_col
    )
    mate_start = (mate_row // SUB) * (lane_tiles * SUB) + mate_row % SUB
    dest = spot // every
    dest_rank = jnp.sum(
        ((dest[:, None] == dest[None, :]) & (spot[None, :] < spot[:, None])).astype(jnp.int32),
        axis=1,
    )
    dest_start = (dest * move_cap + dest_rank) * lane_tiles

    parcels = pl.pallas_call(
        functools.partial(pack_kernel, lane_tiles, block_cols),
        out_shape=jax.ShapeDtypeStruct((dest_count * move_cap * lane_tiles, LANES), jnp.float32),
        in_specs=[pl.BlockSpec(memory_space=pltpu.SMEM)] * 4
        + [pl.BlockSpec(memory_space=pl.ANY)] * 2,
        out_specs=pl.BlockSpec(memory_space=pltpu.VMEM),
        scratch_shapes=[
            pltpu.VMEM(((block_cols + col_count * pair_cap) * lane_tiles, LANES), jnp.float32),
            pltpu.SemaphoreType.DMA((2,)),
        ],
        name="rotate_pack",
    )(mate_start, dest_start, cosine, sine, to_tiles(eigvec_halves), to_tiles(flat_in))
    arrived = lax.all_to_all(
        parcels.reshape(dest_count, move_cap * lane_tiles, LANES),
        ("row", "col"), split_axis=0, concat_axis=0, tiled=True,
    )

    raw = secular_coefficients[:, None] / (secular_singularities[:, None] - secular_zeros[None, :])
    scale_all = lax.rsqrt(jnp.sum(raw * raw, axis=0) + 1e-06)
    by_chip = jnp.stack([secular_zeros, scale_all]).reshape(2, chips, 2, panel_cols // col_count)
    by_chip = jnp.concatenate([by_chip, by_chip], axis=1)
    by_chip = lax.dynamic_slice_in_dim(by_chip, chip, chips, axis=1)

    def partial_panel(parity):
        mine = lax.dynamic_slice_in_dim(by_chip, parity, 1, axis=2).reshape(2, panel_cols // 2)
        zeros, scale = mine[0], mine[1]
        spun = (
            cosine[:, None] * (weight[:, None] / (pole[:, None] - zeros[None, :]))
            - sine[:, None] * (mate_weight[:, None] / (mate_pole[:, None] - zeros[None, :]))
        ) * scale[None, :]
        return lax.dot_general(
            spun, eigvec_halves, (((0,), (0,)), ((), ())),
            precision=lax.Precision.HIGH, preferred_element_type=jnp.float32,
        )

    def shift(array, chip_step):
        pairs = [
            (2 * x + c, 2 * ((x + chip_step) % chips) + c) for x in range(chips) for c in range(2)
        ]
        return lax.ppermute(array, "col", pairs)

    swap = [(c, c ^ 1) for c in range(col_count)]
    partner = lax.ppermute(partial_panel(1 - core), "col", swap)
    both = (partial_panel(core) + partner).reshape(chips, panel_cols // col_count, block_rows)
    half = panel_cols // col_count // 2
    far_up = shift(both[2, :half], 1)
    far_down = shift(both[2, half:], -1)
    up = shift(jnp.concatenate([both[1, :half] + far_up, both[1, half:]]), 1)
    down = shift(jnp.concatenate([both[3, :half], both[3, half:] + far_down]), -1)
    panel = both[0] + up + down

    slot_index = lax.axis_index("row") * col_count + col_index
    wanted = lax.dynamic_slice_in_dim(kept_vectors, slot_index * every, every)
    source = wanted // block_cols
    earlier = jnp.arange(every, dtype=jnp.int32)
    source_rank = jnp.sum(
        ((source[:, None] == source[None, :]) & (earlier[None, :] < earlier[:, None])).astype(
            jnp.int32
        ),
        axis=1,
    )
    starts = (source * move_cap + source_rank) * lane_tiles
    steps = 4
    per_step = row_count // steps
    in_rows = per_step * col_count * move_cap * lane_tiles
    out_rows = per_step * lane_tiles * SUB
    packed = pl.pallas_call(
        functools.partial(unpack_kernel, lane_tiles, col_count, every, per_step),
        grid=(steps,),
        out_shape=jax.ShapeDtypeStruct((every // SUB, row_count * lane_tiles * SUB, LANES), jnp.float32),
        in_specs=[
            pl.BlockSpec(memory_space=pltpu.SMEM),
            pl.BlockSpec((in_rows, LANES), lambda s: (s, 0)),
        ],
        out_specs=pl.BlockSpec((every // SUB, out_rows, LANES), lambda s: (0, s, 0)),
        name="unpack",
    )(starts, arrived.reshape(dest_count * move_cap * lane_tiles, LANES))
    packed_vectors = from_tiles(packed.reshape(-1, LANES), every, row_count * block_rows)
    return (packed_vectors, panel)


def solution(mesh):
    placed = (P("col", "row"), P(), P(), P(), P(), P(), P())
    return jax.shard_map(
        shards,
        mesh=mesh,
        in_specs=placed,
        out_specs=(P(("row", "col"), None), P("col", "row")),
        check_vma=False,
    )
```

time: 193 us -> 127 us (0.66)
  local copies, waits for them, and re-layouts: 57.8 us -> 0.66 us
  matrix products: 29.3 us -> 12 us
  waiting for transfers between devices: 52.1 us -> 68.3 us
  between operations: 14.4 us -> 0.87 us
  Pallas kernels: 0 us -> 13.4 us
  other arithmetic: 20.9 us -> 11 us
  starting transfers between devices: 16.9 us -> 19.7 us
    ppermute x0 -> x5, waiting for transfers between devices: none -> 57.8 us  [the longest x4 57.8 us: shift(): return lax.ppermute(array, 'col', pairs)]
    all_to_all x1, waiting for transfers between devices: 52.1 us -> 0.01 us  [shards(): lax.all_to_all(parcels.reshape(dest_count, move_cap * lane_tiles, LANES),...]
    gather x26 -> x0, local copies, waits for them, and re-layouts: 41.3 us -> none  [the longest x18 20.5 us: bucket_table(): edge_ids = jnp.searchsorted(sorted_keys, boundary_keys)]
    dot_general x6 -> x3, matrix products: 29.3 us -> 12 us  [the longest x2 7.24 us: partial_panel(): lax.dot_general(spun, eigvec_halves, (((0,), (0,)), ((), ())), precision=...]
    pallas_call x0 -> x2, Pallas kernels: none -> 13.4 us  [the longest x1 8.69 us: shards(): pl.pallas_call(functools.partial(pack_kernel, lane_tiles, block_cols), ou...]
    sort x3 -> x0, other arithmetic: 13.3 us -> none  [the longest x2 7.55 us: bucket_table(): ordering = jnp.argsort(sort_keys, stable=True)]
    reshape x2 -> x0, local copies, waits for them, and re-layouts: 10.5 us -> none  [the longest x1 5.29 us: shards(): arrived = arrived.reshape(row_count, col_count * move_cap, block_rows)]
    all_to_all x1, waiting for transfers between devices: 0.01 us -> 10.5 us  [shards(): lax.all_to_all(outgoing, 'col', split_axis=0, concat_axis=0, tiled=True)]
  transfers between devices with their start and end apart: 3 -> 7, of which waited for: 1 -> 4; matrix products, arithmetic and copies ran while one was open for 37% -> 13% of each run, Pallas kernels for 0% -> 7%
where the time goes in v1:
time: 127 us; the launch traced here: 126 us
  waiting for transfers between devices  68.3 us (54%)
  starting transfers between devices  19.7 us (16%)
  Pallas kernels  13.4 us (11%)
  matrix products  12 us (9%)
  other arithmetic  11 us (9%)
    ppermute x4, waiting for transfers between devices, shift(): return lax.ppermute(array, 'col', pairs)  57.8 us
    all_to_all x1, waiting for transfers between devices, shards(): lax.all_to_all(outgoing, 'col', split_axis=0, concat_axis=0, tiled=True)  10.5 us
    all_to_all x1, starting transfers between devices, shards(): lax.all_to_all(parcels.reshape(dest_count, move_cap * lane_tiles, LANES),...  9.58 us
    pallas_call x1, Pallas kernels, shards(): pl.pallas_call(functools.partial(pack_kernel, lane_tiles, block_cols), ou...  8.69 us
    dot_general x2, matrix products, partial_panel(): lax.dot_general(spun, eigvec_halves, (((0,), (0,)), ((), ())), precision=...  7.24 us
    all_to_all x1, starting transfers between devices, shards(): lax.all_to_all(outgoing, 'col', split_axis=0, concat_axis=0, tiled=True)  5.79 us
    dot_general x1, matrix products, shards(): jnp.dot(pick, eigvec_halves, precision=lax.Precision.HIGHEST, preferred_e...  4.8 us
    pallas_call x1, Pallas kernels, shards(): pl.pallas_call(functools.partial(unpack_kernel, lane_tiles, col_count, ev...  4.69 us
  transfers between devices with their start and end apart: 7, of which 4 were waited for; matrix products, arithmetic and copies ran while one was open for 13% of the time, Pallas kernels for 7%

profile of v1, /device:TPU:1, one launch (start us, length us, event | category | flops | bytes accessed | tf_op | source)
XLA Modules:
  0.0 126.0 jit_solution(6136508500370784157)
XLA Ops:
  0.6 0.0 copy-start
  0.6 0.0 copy-start.10
  0.7 0.0 copy-start.11
  0.7 0.0 copy-start.4
  0.7 0.0 copy-start.5
  0.7 0.0 copy-start.3
  0.7 0.9 fusion.47
  1.6 0.3 convert_reduce_fusion
  2.0 0.6 add_select_fusion.4
  2.6 4.8 %fusion.23 = f32[192,2048]{1,0:T(8,128)} fusion(f32[384,2048]{1,0:T(8,128)} %param.7, s32[384]{0:T(512)S(1)} %get-tuple-element.24), kind=kOutput, calls=%fused_computation.42 | convolution fusion | flops 1812013056 | bytes 4720128 | tf_op jit(solution)/shard_map/dot_general | solution.py:104
  7.4 5.8 %all-to-all-start = ((f32[8,24,2048]{2,1,0:T(8,128)}), f32[8,24,2048]{2,1,0:T(8,128)}, u32[]{:S(2)}, u32[]{:S(2)}) async-start(f32[8,24,2048]{2,1,0:T(8,128)} %bitcast.42), calls=%async_computation | async-start | bytes 3145728 | tf_op jit(solution)/shard_map/all_to_all | solution.py:107
  13.2 0.7 select_reduce_fusion
  14.0 0.1 stack.7
  14.1 1.7 %multiply_reduce_fusion = f32[512]{0:T(512)S(1)} fusion(f32[512]{0:T(512)S(1)} %copy-done.11, f32[3072]{0:T(1024)S(1)} %copy-done.4, f32[3072]{0:T(1024)S(1)} %copy-done.5), kind=kLoop, calls=%fused_computation.3 | loop fusion | flops 6290944 | bytes 28672 | tf_op jit(solution)/shard_map/reduce_sum | solution.py:154
  15.8 0.1 rsqrt.15
  15.9 0.1 mul.114
  16.0 0.1 sub.116
  16.1 2.1 %fusion.4 = (f32[384]{0:T(512)S(1)}, f32[384]{0:T(512)S(1)}, f32[384]{0:T(512)S(1)}, f32[384]{0:T(512)S(1)}) fusion(f32[3072]{0:T(1024)S(1)} %copy-done.4, s32[3072]{0:T(1024)S(1)} %copy-done.3, s32[384]{0:T(512)S(1)} %get-tuple-element.26, s32[384]{0:T(512)S(1)} %get-tuple-element.15, f32[3072]{0:T(1024)S(1)} %copy-done.5), kind=kLoop, calls=%fused_computation.10 | loop fusion | flops 11794944 | bytes 46080 | tf_op jit(solution)/shard_map/reduce_sum | solution.py:68
  18.3 3.5 %fusion.6 = f32[256,2048]{1,0:T(8,128)} fusion(f32[384,2048]{1,0:T(8,128)S(1)} %copy-done, f32[256]{0:T(256)S(1)} %mul.114, f32[256]{0:T(256)S(1)} %sub.116, f32[384]{0:T(512)S(1)} %get-tuple-element.5, f32[384]{0:T(512)S(1)} %get-tuple-element.6, f32[384]{0:T(512)S(1)} %get-tuple-element.22.sin_ref, f32[384]{0:T(512)S(1)} %get-tuple-element.4, ...), kind=kOutput, calls=%fused_computation.24 | convolution fusion | flops 1208745984 | bytes 5254144 | tf_op jit(solution)/shard_map/dot_general | solution.py:166
  21.7 0.0 collective-permute-start
  21.7 0.7 fusion.2
  22.5 0.3 convert_reduce_fusion.1
  22.7 0.6 add_multiply_fusion.dest_ref
  23.4 10.5 %all-to-all-done = f32[8,24,2048]{2,1,0:T(8,128)} async-done(((f32[8,24,2048]{2,1,0:T(8,128)}), f32[8,24,2048]{2,1,0:T(8,128)}, u32[]{:S(2)}, u32[]{:S(2)}) %all-to-all-start) | async-done | bytes 1572896 | tf_op jit(solution)/shard_map/all_to_all | solution.py:107
  33.9 8.7 %rotate_pack.1 = f32[8192,128]{1,0:T(8,128)} custom-call(s32[384]{0:T(512)} %get-tuple-element.25.mate_ref, s32[384]{0:T(512)} %add_multiply_fusion.dest_ref, f32[384]{0:T(512)} %copy-done.8, f32[384]{0:T(512)} %copy-done.6, f32[6144,128]{1,0:T(8,128)} %bitcast.38, f32[3072,128]{1,0:T(8,128)} %bitcast.6.mates_hbm), custom_call_target="tpu_custom_call" | custom-call | tf_op jit(solution)/shard_map/rotate_pack/pallas_call | solution.py:136
  42.6 0.0 copy-start.1
  42.6 9.6 %all-to-all-start.1 = ((f32[128,64,128]{2,1,0:T(8,128)}), f32[128,64,128]{2,1,0:T(8,128)}, u32[]{:S(2)}, u32[]{:S(2)}) async-start(f32[128,64,128]{2,1,0:T(8,128)} %bitcast.39), calls=%async_computation.1 | async-start | bytes 8388608 | tf_op jit(solution)/shard_map/all_to_all | solution.py:148
  52.2 0.1 mul.109
  52.3 0.1 sub.109
  52.4 0.0 collective-permute-done
  52.4 3.8 %convolution_add_fusion = f32[256,2048]{1,0:T(8,128)S(1)} fusion(f32[256,2048]{1,0:T(8,128)} %collective-permute-done, f32[384,2048]{1,0:T(8,128)S(1)} %copy-done.1, f32[256]{0:T(256)S(1)} %mul.109, f32[384]{0:T(512)S(1)} %get-tuple-element.5, f32[384]{0:T(512)S(1)} %get-tuple-element.6, f32[384]{0:T(512)S(1)} %copy-done.7, f32[256]{0:T(256)S(1)} %sub.109, ...), kind=kOutput, calls=%fused_computation.13 | convolution fusion | flops 1209270272 | bytes 7351296 | tf_op jit(solution)/shard_map/dot_general | solution.py:166
  56.2 0.0 copy-start.2
  56.2 0.1 slice_bitcast_fusion.4
  56.3 1.4 %collective-permute-start.1 = (f32[32,2048]{1,0:T(8,128)S(1)}, f32[32,2048]{1,0:T(8,128)S(1)}, u32[]{:S(2)}, u32[]{:S(2)}) collective-permute-start(f32[32,2048]{1,0:T(8,128)S(1)} %get-tuple-element.18), channel_id=1, source_target_pairs={{0,2},{1,3},{2,4},{3,5},{4,6},{5,7},{6,0},{7,1},{8,10},{9,11},{10,... | collective-permute-start | bytes 786440 | tf_op jit(solution)/shard_map/ppermute | solution.py:175
  57.7 1.3 %collective-permute-start.3 = (f32[32,2048]{1,0:T(8,128)S(1)}, f32[32,2048]{1,0:T(8,128)S(1)}, u32[]{:S(2)}, u32[]{:S(2)}) collective-permute-start(f32[32,2048]{1,0:T(8,128)S(1)} %get-tuple-element.19), channel_id=1, source_target_pairs={{0,6},{1,7},{2,0},{3,1},{4,2},{5,3},{6,4},{7,5},{8,14},{9,15},{10,... | collective-permute-start | bytes 786440 | tf_op jit(solution)/shard_map/ppermute | solution.py:175
  59.0 46.0 %collective-permute-done.1 = f32[32,2048]{1,0:T(8,128)S(1)} collective-permute-done((f32[32,2048]{1,0:T(8,128)S(1)}, f32[32,2048]{1,0:T(8,128)S(1)}, u32[]{:S(2)}, u32[]{:S(2)}) %collective-permute-start.1) | collective-permute-done | bytes 262176 | tf_op jit(solution)/shard_map/ppermute | solution.py:175
  105.0 0.0 collective-permute-done.3
  105.0 0.1 fusion.25
  105.1 0.6 collective-permute-start.4
  105.8 1.0 collective-permute-start.2
  106.7 0.1 and_select_fusion
  106.8 0.2 convert_reduce_fusion.3
  107.0 0.6 add_multiply_fusion.1.start_ref
  107.6 10.2 %collective-permute-done.4 = f32[64,2048]{1,0:T(8,128)S(1)} collective-permute-done((f32[64,2048]{1,0:T(8,128)S(1)}, f32[64,2048]{1,0:T(8,128)S(1)}, u32[]{:S(2)}, u32[]{:S(2)}) %collective-permute-start.4) | collective-permute-done | bytes 524320 | tf_op jit(solution)/shard_map/ppermute | solution.py:175
  117.8 1.6 %collective-permute-done.2 = f32[64,2048]{1,0:T(8,128)S(1)} collective-permute-done((f32[64,2048]{1,0:T(8,128)S(1)}, f32[64,2048]{1,0:T(8,128)S(1)}, u32[]{:S(2)}, u32[]{:S(2)}) %collective-permute-start.2) | collective-permute-done | bytes 524320 | tf_op jit(solution)/shard_map/ppermute | solution.py:175
  119.4 1.9 %fusion.5 = f32[64,2048]{1,0:T(8,128)} fusion(f32[64,2048]{1,0:T(8,128)S(1)} %collective-permute-done.4, f32[64,2048]{1,0:T(8,128)S(1)} %collective-permute-done.2, f32[256,2048]{1,0:T(8,128)} %copy-done.2), kind=kLoop, calls=%fused_computation.21 | loop fusion | flops 262144 | bytes 2097152 | tf_op jit(solution)/shard_map/add | solution.py:185
  121.3 0.0 all-to-all-done.1
  121.3 4.7 %unpack.1 = f32[3,2048,128]{2,1,0:T(8,128)} custom-call(s32[24]{0:T(128)} %add_multiply_fusion.1.start_ref, f32[8192,128]{1,0:T(8,128)} %bitcast.8.in_ref), custom_call_target="tpu_custom_call" | custom-call | tf_op jit(solution)/shard_map/unpack/pallas_call | solution.py:202
  (24 shorter events, 0.2 us)
Async XLA Ops:
  0.6 17.6 %copy-start = (f32[384,2048]{1,0:T(8,128)S(1)}, f32[384,2048]{1,0:T(8,128)}, u32[]{:S(2)}) copy-start(f32[384,2048]{1,0:T(8,128)} %param.7) | copy-start | bytes 9437188
  0.6 12.5 %copy-start.10 = (f32[3072]{0:T(1024)S(1)}, f32[3072]{0:T(1024)}, u32[]{:S(2)}) copy-start(f32[3072]{0:T(1024)} %param.9) | copy-start | bytes 36868
  0.7 13.3 %copy-start.11 = (f32[512]{0:T(512)S(1)}, f32[512]{0:T(512)}, u32[]{:S(2)}) copy-start(f32[512]{0:T(512)} %param.13) | copy-start | bytes 6148
  0.7 13.4 %copy-start.4 = (f32[3072]{0:T(1024)S(1)}, f32[3072]{0:T(1024)}, u32[]{:S(2)}) copy-start(f32[3072]{0:T(1024)} %param.11) | copy-start | bytes 36868
  0.7 13.4 %copy-start.5 = (f32[3072]{0:T(1024)S(1)}, f32[3072]{0:T(1024)}, u32[]{:S(2)}) copy-start(f32[3072]{0:T(1024)} %param.12) | copy-start | bytes 36868
  0.7 15.4 %copy-start.3 = (s32[3072]{0:T(1024)S(1)}, s32[3072]{0:T(1024)}, u32[]{:S(2)}) copy-start(s32[3072]{0:T(1024)} %param.10) | copy-start | bytes 36868
  7.4 26.5 %all-to-all-start = ((f32[8,24,2048]{2,1,0:T(8,128)}), f32[8,24,2048]{2,1,0:T(8,128)}, u32[]{:S(2)}, u32[]{:S(2)}) async-start(f32[8,24,2048]{2,1,0:T(8,128)} %bitcast.42), calls=%async_computation | async-start | bytes 3145728 | tf_op jit(solution)/shard_map/all_to_all | solution.py:107
  14.0 19.9 %copy-start.6 = (f32[384]{0:T(512)}, f32[384]{0:T(512)S(1)}, u32[]{:S(2)}) copy-start(f32[384]{0:T(512)S(1)} %get-tuple-element.22.sin_ref) | copy-start | bytes 4612
  14.0 19.9 %copy-start.8 = (f32[384]{0:T(512)}, f32[384]{0:T(512)S(1)}, u32[]{:S(2)}) copy-start(f32[384]{0:T(512)S(1)} %get-tuple-element.23.cos_ref) | copy-start | bytes 4612
  21.7 30.7 %collective-permute-start = (f32[256,2048]{1,0:T(8,128)}, f32[256,2048]{1,0:T(8,128)}, u32[]{:S(2)}, u32[]{:S(2)}) collective-permute-start(f32[256,2048]{1,0:T(8,128)} %fusion.6), channel_id=1, source_target_pairs={{0,1},{1,0},{2,3},{3,2},{4,5},{5,4},{6,7},{7,6},{8,9},{9,8},{10,11... | collective-permute-start | bytes 6291464 | tf_op jit(solution)/shard_map/ppermute | solution.py:178
  42.6 9.8 %copy-start.1 = (f32[384,2048]{1,0:T(8,128)S(1)}, f32[384,2048]{1,0:T(8,128)}, u32[]{:S(2)}) copy-start(f32[384,2048]{1,0:T(8,128)} %param.7) | copy-start | bytes 9437188
  42.6 9.8 %copy-start.7 = (f32[384]{0:T(512)S(1)}, f32[384]{0:T(512)}, u32[]{:S(2)}) copy-start(f32[384]{0:T(512)} %copy-done.6) | copy-start | bytes 4612
  42.6 9.8 %copy-start.9 = (f32[384]{0:T(512)S(1)}, f32[384]{0:T(512)}, u32[]{:S(2)}) copy-start(f32[384]{0:T(512)} %copy-done.8) | copy-start | bytes 4612
  42.6 78.7 %all-to-all-start.1 = ((f32[128,64,128]{2,1,0:T(8,128)}), f32[128,64,128]{2,1,0:T(8,128)}, u32[]{:S(2)}, u32[]{:S(2)}) async-start(f32[128,64,128]{2,1,0:T(8,128)} %bitcast.39), calls=%async_computation.1 | async-start | bytes 8388608 | tf_op jit(solution)/shard_map/all_to_all | solution.py:148
  56.2 48.8 %copy-start.2 = (f32[256,2048]{1,0:T(8,128)}, f32[256,2048]{1,0:T(8,128)S(1)}, u32[]{:S(2)}) copy-start(f32[256,2048]{1,0:T(8,128)S(1)} %convolution_add_fusion) | copy-start | bytes 6291460
  56.3 48.7 %collective-permute-start.1 = (f32[32,2048]{1,0:T(8,128)S(1)}, f32[32,2048]{1,0:T(8,128)S(1)}, u32[]{:S(2)}, u32[]{:S(2)}) collective-permute-start(f32[32,2048]{1,0:T(8,128)S(1)} %get-tuple-element.18), channel_id=1, source_target_pairs={{0,2},{1,3},{2,4},{3,5},{4,6},{5,7},{6,0},{7,1},{8,10},{9,11},{10,... | collective-permute-start | bytes 786440 | tf_op jit(solution)/shard_map/ppermute | solution.py:175
  57.7 47.3 %collective-permute-start.3 = (f32[32,2048]{1,0:T(8,128)S(1)}, f32[32,2048]{1,0:T(8,128)S(1)}, u32[]{:S(2)}, u32[]{:S(2)}) collective-permute-start(f32[32,2048]{1,0:T(8,128)S(1)} %get-tuple-element.19), channel_id=1, source_target_pairs={{0,6},{1,7},{2,0},{3,1},{4,2},{5,3},{6,4},{7,5},{8,14},{9,15},{10,... | collective-permute-start | bytes 786440 | tf_op jit(solution)/shard_map/ppermute | solution.py:175
  105.1 12.7 %collective-permute-start.4 = (f32[64,2048]{1,0:T(8,128)S(1)}, f32[64,2048]{1,0:T(8,128)S(1)}, u32[]{:S(2)}, u32[]{:S(2)}) collective-permute-start(f32[64,2048]{1,0:T(8,128)S(1)} %pad_maximum_fusion.1), channel_id=1, source_target_pairs={{0,6},{1,7},{2,0},{3,1},{4,2},{5,3},{6,4},{7,5},{8,14},{9,15},{10,... | collective-permute-start | bytes 1572872 | tf_op jit(solution)/shard_map/ppermute | solution.py:175
  105.8 13.6 %collective-permute-start.2 = (f32[64,2048]{1,0:T(8,128)S(1)}, f32[64,2048]{1,0:T(8,128)S(1)}, u32[]{:S(2)}, u32[]{:S(2)}) collective-permute-start(f32[64,2048]{1,0:T(8,128)S(1)} %pad_maximum_fusion), channel_id=1, source_target_pairs={{0,2},{1,3},{2,4},{3,5},{4,6},{5,7},{6,0},{7,1},{8,10},{9,11},{10,... | collective-permute-start | bytes 1572872 | tf_op jit(solution)/shard_map/ppermute | solution.py:175

commit v2 on v1

v2 whole, which is shorter than its diff:
```python
import functools

import jax
import jax.numpy as jnp
from jax import lax
from jax.experimental import pallas as pl
from jax.experimental.pallas import tpu as pltpu
from jax.sharding import PartitionSpec as P


LANES = 128
SUB = 8
GROUP = 8


def tile_view(rows):
    count, width = rows.shape
    tiles = rows.reshape(count // SUB, SUB, width // LANES, LANES).transpose(0, 2, 1, 3)
    return tiles.reshape(count // SUB, width // LANES * SUB, LANES)


def from_tiles(tiles, count, width):
    rows = tiles.reshape(count // SUB, width // LANES, SUB, LANES)
    return rows.transpose(0, 2, 1, 3).reshape(count, width)


def send_kernel(pair_cap, pieces, first_ref, mates_hbm, tiles_hbm, out_hbm,
                mates_ref, tiles_ref, stage_ref, slots_ref, source_ref, sems):
    table = pltpu.make_async_copy(mates_hbm, mates_ref, sems.at[1])
    table.start()
    load = pltpu.make_async_copy(tiles_hbm, tiles_ref, sems.at[0])
    load.start()
    columns, parts = tiles_ref.shape[0] * SUB, stage_ref.shape[1] // SUB
    table.wait()
    count = stage_ref.shape[0]
    blocks = count // pair_cap
    local = columns // LANES
    local_mates = mates_ref[pl.ds(first_ref[0] * local, local), :]
    owner = jnp.concatenate([local_mates[i : i + 1] for i in range(local)], axis=1) // columns
    member = lax.broadcasted_iota(jnp.int32, (blocks, columns), 0) == owner
    earlier = lax.broadcasted_iota(jnp.int32, (columns, columns), 0) < lax.broadcasted_iota(
        jnp.int32, (columns, columns), 1
    )
    before = jnp.dot(
        member.astype(jnp.bfloat16), earlier.astype(jnp.bfloat16),
        preferred_element_type=jnp.float32,
    )
    rank = jnp.sum(jnp.where(member, before, 0.0), axis=0, keepdims=True).astype(jnp.int32)
    place = jnp.where(rank < pair_cap, owner * pair_cap + rank, -1)
    pick = (
        lax.broadcasted_iota(jnp.int32, (count, columns), 0) == place
    ).astype(jnp.bfloat16)
    order = lax.broadcasted_iota(jnp.int32, (SUB, columns), 1)
    digit = lax.broadcasted_iota(jnp.int32, (SUB, columns), 0)
    digits = jnp.where(digit == 0, order // LANES, order % LANES).astype(jnp.bfloat16)
    found = lax.dot_general(
        digits, pick, (((1,), (1,)), ((), ())), preferred_element_type=jnp.float32
    )
    slots_ref[...] = (found[0:1] * LANES + found[1:2]).astype(jnp.int32)
    indices = pltpu.make_async_copy(slots_ref, source_ref, sems.at[1])
    indices.start()
    load.wait()

    indices.wait()

    def group(g, carry):
        values = []
        for n in range(GROUP):
            source = source_ref[0, g * GROUP + n]
            values += [
                tiles_ref[source // SUB, pl.ds(part * SUB * SUB + source % SUB, SUB, SUB), :]
                for part in range(parts)
            ]
        for n, value in enumerate(values):
            stage_ref[g * GROUP + n // parts, pl.ds(n % parts * SUB, SUB), :] = value
        return carry

    piece = count // pieces
    stores = []
    for n in range(pieces):
        lax.fori_loop(n * piece // GROUP, (n + 1) * piece // GROUP, group, 0, unroll=2)
        store = pltpu.make_async_copy(
            stage_ref.at[pl.ds(n * piece, piece)], out_hbm.at[pl.ds(n * piece, piece)], sems.at[2 + n]
        )
        store.start()
        stores.append(store)
    for store in stores:
        store.wait()


def pack_kernel(pieces, source_ref, mate_ref, cos_ref, sin_ref, tiles_hbm, mates_hbm, out_hbm,
                tiles_ref, rows_ref, stage_ref, load_sems, store_sems):
    local_rows, parts = tiles_ref.shape[0] * SUB, rows_ref.shape[1] // SUB
    own_load = pltpu.make_async_copy(tiles_hbm, tiles_ref, load_sems.at[0])
    mate_load = pltpu.make_async_copy(
        mates_hbm, rows_ref.at[pl.ds(local_rows, mates_hbm.shape[0])], load_sems.at[1]
    )
    own_load.start()
    mate_load.start()
    own_load.wait()

    def spread(g, carry):
        values = [
            tiles_ref[g, pl.ds(part * SUB * SUB + s, SUB, SUB), :]
            for s in range(SUB) for part in range(parts)
        ]
        for n, value in enumerate(values):
            rows_ref[g * SUB + n // parts, pl.ds(n % parts * SUB, SUB), :] = value
        return carry

    lax.fori_loop(0, tiles_ref.shape[0], spread, 0, unroll=2)
    mate_load.wait()

    def group(g, carry):
        sources = [source_ref[g * GROUP + n] for n in range(GROUP)]
        values = [cos_ref[i] * rows_ref[i] + sin_ref[i] * rows_ref[mate_ref[i]] for i in sources]
        for n, value in enumerate(values):
            stage_ref[g * GROUP + n] = value
        return carry

    piece = stage_ref.shape[0] // pieces
    stores = []
    for n in range(pieces):
        lax.fori_loop(n * piece // GROUP, (n + 1) * piece // GROUP, group, 0, unroll=2)
        part = pl.ds(n * piece, piece)
        store = pltpu.make_async_copy(stage_ref.at[part], out_hbm.at[part], store_sems.at[n])
        store.start()
        stores.append(store)
    for store in stores:
        store.wait()


def unpack_kernel(wanted, per_step, start_ref, in_ref, out_ref):
    slots = in_ref.shape[0] // per_step
    parts = in_ref.shape[1] // SUB
    for r in range(per_step):
        for first in range(0, wanted, SUB):
            values = [in_ref[start_ref[first + n] + r * slots] for n in range(SUB)]
            for n, value in enumerate(values):
                for part in range(parts):
                    out_ref[first // SUB, r, pl.ds(part * SUB * SUB + n, SUB, SUB), :] = value[
                        part * SUB : (part + 1) * SUB
                    ]


def one_hot_sum(match, values):
    return jnp.sum(jnp.where(match, values[None, :], jnp.zeros((), values.dtype)), axis=1)


def shards(
    eigvec_halves,
    rotation_mate,
    givens_theta,
    kept_vectors,
    secular_singularities,
    secular_coefficients,
    secular_zeros,
):
    col_count = lax.axis_size("col")
    row_count = lax.axis_size("row")
    chips = col_count // 2
    block_cols, block_rows = eigvec_halves.shape
    total_cols = rotation_mate.shape[0]
    panel_cols = secular_zeros.shape[0]
    pair_cap = block_cols // 16
    lane_tiles = block_rows // LANES
    dest_count = row_count * col_count
    every = total_cols // dest_count
    move_cap = every // col_count + every // col_count // 3
    col_index = lax.axis_index("col")
    chip, core = col_index // 2, col_index % 2
    first_col = col_index * block_cols

    order = jnp.arange(block_cols, dtype=jnp.int32)
    labels = first_col + order
    mates = lax.dynamic_slice_in_dim(rotation_mate, first_col, block_cols)
    owner = mates // block_cols
    same_owner = owner[:, None] == owner[None, :]
    tiles = tile_view(eigvec_halves)
    slot_count = col_count * pair_cap
    pieces = 4
    outgoing = pl.pallas_call(
        functools.partial(send_kernel, pair_cap, pieces),
        out_shape=jax.ShapeDtypeStruct((slot_count, lane_tiles, LANES), jnp.float32),
        in_specs=[pl.BlockSpec(memory_space=pltpu.SMEM)] + [pl.BlockSpec(memory_space=pl.ANY)] * 2,
        out_specs=pl.BlockSpec(memory_space=pl.ANY),
        scratch_shapes=[
            pltpu.VMEM((total_cols // LANES, LANES), jnp.int32),
            pltpu.VMEM(tiles.shape, jnp.float32),
            pltpu.VMEM((slot_count, lane_tiles, LANES), jnp.float32),
            pltpu.VMEM((1, slot_count), jnp.int32),
            pltpu.SMEM((1, slot_count), jnp.int32),
            pltpu.SemaphoreType.DMA((2 + pieces,)),
        ],
        name="send",
    )(col_index[None], rotation_mate.reshape(-1, LANES), tiles)
    incoming = lax.all_to_all(outgoing, "col", split_axis=0, concat_axis=0, tiled=True)

    paired = mates != labels
    own_match = kept_vectors[None, :] == labels[:, None]
    mate_match = kept_vectors[None, :] == mates[:, None]
    positions = jnp.arange(total_cols, dtype=jnp.int32)
    spot = one_hot_sum(own_match, positions)
    pole = one_hot_sum(own_match, secular_singularities)
    weight = one_hot_sum(own_match, secular_coefficients)
    mate_pole = one_hot_sum(mate_match, secular_singularities)
    mate_weight = one_hot_sum(mate_match, secular_coefficients)
    angle = one_hot_sum(positions[None, :] == jnp.minimum(labels, mates)[:, None], givens_theta)
    sign_flip = jnp.where(labels < mates, -1.0, 1.0).astype(jnp.float32)
    cosine = jnp.where(paired, jnp.cos(angle), 1.0)
    sine = jnp.where(paired, sign_flip * jnp.sin(angle), 0.0)

    recv_rank = jnp.sum((same_owner & (mates[None, :] < mates[:, None])).astype(jnp.int32), axis=1)
    remote = owner != col_index
    mate_row = jnp.where(remote, block_cols + owner * pair_cap + recv_rank, mates - first_col)
    dest = spot // every
    dest_rank = jnp.sum(
        ((dest[:, None] == dest[None, :]) & (spot[None, :] < spot[:, None])).astype(jnp.int32),
        axis=1,
    )
    dest_slot = dest * move_cap + dest_rank
    places = dest_count * move_cap
    filled = dest_slot[None, :] == jnp.arange(places, dtype=jnp.int32)[:, None]
    place_source = one_hot_sum(filled, order)
    parcels = pl.pallas_call(
        functools.partial(pack_kernel, pieces),
        out_shape=jax.ShapeDtypeStruct((places, lane_tiles, LANES), jnp.float32),
        in_specs=[pl.BlockSpec(memory_space=pltpu.SMEM)] * 4
        + [pl.BlockSpec(memory_space=pl.ANY)] * 2,
        out_specs=pl.BlockSpec(memory_space=pl.ANY),
        scratch_shapes=[
            pltpu.VMEM(tiles.shape, jnp.float32),
            pltpu.VMEM((block_cols + slot_count, lane_tiles, LANES), jnp.float32),
            pltpu.VMEM((places, lane_tiles, LANES), jnp.float32),
            pltpu.SemaphoreType.DMA((2,)),
            pltpu.SemaphoreType.DMA((pieces,)),
        ],
        name="rotate_pack",
    )(place_source, mate_row, cosine, sine, tiles, incoming)
    arrived = lax.all_to_all(
        parcels.reshape(dest_count, move_cap * lane_tiles, LANES),
        ("row", "col"), split_axis=0, concat_axis=0, tiled=True,
    )

    raw = secular_coefficients[:, None] / (secular_singularities[:, None] - secular_zeros[None, :])
    scale_all = lax.rsqrt(jnp.sum(raw * raw, axis=0) + 1e-06)
    by_chip = jnp.stack([secular_zeros, scale_all]).reshape(2, chips, 2, panel_cols // col_count)
    by_chip = jnp.concatenate([by_chip, by_chip], axis=1)
    by_chip = lax.dynamic_slice_in_dim(by_chip, chip, chips, axis=1)

    def partial_panel(parity):
        mine = lax.dynamic_slice_in_dim(by_chip, parity, 1, axis=2).reshape(2, panel_cols // 2)
        zeros, scale = mine[0], mine[1]
        spun = (
            cosine[:, None] * (weight[:, None] / (pole[:, None] - zeros[None, :]))
            - sine[:, None] * (mate_weight[:, None] / (mate_pole[:, None] - zeros[None, :]))
        ) * scale[None, :]
        return lax.dot_general(
            spun, eigvec_halves, (((0,), (0,)), ((), ())),
            precision=lax.Precision.HIGH, preferred_element_type=jnp.float32,
        )

    def shift(array, chip_step):
        pairs = [
            (2 * x + c, 2 * ((x + chip_step) % chips) + c) for x in range(chips) for c in range(2)
        ]
        return lax.ppermute(array, "col", pairs)

    swap = [(c, c ^ 1) for c in range(col_count)]
    theirs = partial_panel(1 - core)
    partner = lax.ppermute(theirs, "col", swap)
    both = (partial_panel(core) + partner).reshape(chips, panel_cols // col_count, block_rows)
    half = panel_cols // col_count // 2
    far_up = shift(both[2, :half], 1)
    far_down = shift(both[2, half:], -1)
    up = shift(jnp.concatenate([both[1, :half] + far_up, both[1, half:]]), 1)
    down = shift(jnp.concatenate([both[3, :half], both[3, half:] + far_down]), -1)

    slot_index = lax.axis_index("row") * col_count + col_index
    wanted = lax.dynamic_slice_in_dim(kept_vectors, slot_index * every, every)
    source = wanted // block_cols
    earlier = jnp.arange(every, dtype=jnp.int32)
    source_rank = jnp.sum(
        ((source[:, None] == source[None, :]) & (earlier[None, :] < earlier[:, None])).astype(
            jnp.int32
        ),
        axis=1,
    )
    starts = source * move_cap + source_rank
    steps = 4
    per_step = row_count // steps
    packed = pl.pallas_call(
        functools.partial(unpack_kernel, every, per_step),
        grid=(steps,),
        out_shape=jax.ShapeDtypeStruct(
            (every // SUB, row_count, lane_tiles * SUB, LANES), jnp.float32
        ),
        in_specs=[
            pl.BlockSpec(memory_space=pltpu.SMEM),
            pl.BlockSpec(
                (per_step * col_count * move_cap, lane_tiles, LANES), lambda s: (s, 0, 0)
            ),
        ],
        out_specs=pl.BlockSpec(
            (every // SUB, per_step, lane_tiles * SUB, LANES), lambda s: (0, s, 0, 0)
        ),
        name="unpack",
    )(starts, arrived.reshape(dest_count * move_cap, lane_tiles, LANES))
    packed_vectors = from_tiles(packed.reshape(-1, LANES), every, row_count * block_rows)
    packed_vectors, up, down = lax.optimization_barrier((packed_vectors, up, down))
    panel = both[0] + up + down
    return (packed_vectors, panel)


def solution(mesh):
    placed = (P("col", "row"), P(), P(), P(), P(), P(), P())

    return jax.shard_map(
        shards,
        mesh=mesh,
        in_specs=placed,
        out_specs=(P(("row", "col"), None), P("col", "row")),
        check_vma=False,
    )
```

time: 127 us -> 116 us (0.913)
  waiting for transfers between devices: 68.3 us -> 60.4 us
  matrix products: 12 us -> 7.23 us
    ppermute x4, waiting for transfers between devices: 57.8 us -> 51.7 us  [shift(): return lax.ppermute(array, 'col', pairs)]
    dot_general x1 -> x0, matrix products: 4.8 us -> none  [shards(): jnp.dot(pick, eigvec_halves, precision=lax.Precision.HIGHEST, preferred_e...]
    all_to_all x1, waiting for transfers between devices: 10.5 us -> 8.71 us  [shards(): lax.all_to_all(outgoing, 'col', split_axis=0, concat_axis=0, tiled=True)]
    pallas_call x2 -> x3, Pallas kernels: 13.4 us -> 14.6 us  [the longest x1 5.85 us: shards(): pl.pallas_call(functools.partial(pack_kernel, pieces), out_shape=jax.Shap...]
    reduce_sum x3 -> x4, other arithmetic: 3.63 us -> 4.39 us  [one_hot_sum(): jnp.sum(jnp.where(match, values[None, :], jnp.zeros((), values.dtype)), a...]
  transfers between devices with their start and end apart: 7 -> 7, of which waited for: 4 -> 4; matrix products, arithmetic and copies ran while one was open for 13% -> 15% of each run, Pallas kernels for 7% -> 9%
where the time goes in v2:
time: 116 us
  waiting for transfers between devices  60.4 us (52%)
  starting transfers between devices  20.8 us (18%)
  Pallas kernels  14.6 us (13%)
  other arithmetic  11 us (9%)
  matrix products  7.23 us (6%)
    ppermute x4, waiting for transfers between devices, shift(): return lax.ppermute(array, 'col', pairs)  51.7 us
    all_to_all x1, starting transfers between devices, shards(): lax.all_to_all(parcels.reshape(dest_count, move_cap * lane_tiles, LANES),...  9.57 us
    all_to_all x1, waiting for transfers between devices, shards(): lax.all_to_all(outgoing, 'col', split_axis=0, concat_axis=0, tiled=True)  8.71 us
    dot_general x2, matrix products, partial_panel(): lax.dot_general(spun, eigvec_halves, (((0,), (0,)), ((), ())), precision=...  7.23 us
    pallas_call x1, Pallas kernels, shards(): pl.pallas_call(functools.partial(pack_kernel, pieces), out_shape=jax.Shap...  5.85 us
    all_to_all x1, starting transfers between devices, shards(): lax.all_to_all(outgoing, 'col', split_axis=0, concat_axis=0, tiled=True)  5.8 us
    ppermute x4, starting transfers between devices, shift(): return lax.ppermute(array, 'col', pairs)  5.44 us
    pallas_call x1, Pallas kernels, shards(): pl.pallas_call(functools.partial(unpack_kernel, every, per_step), grid=(s...  4.59 us
  transfers between devices with their start and end apart: 7, of which 4 were waited for; matrix products, arithmetic and copies ran while one was open for 15% of the time, Pallas kernels for 9%

profile of v2, /device:TPU:1, one launch (start us, length us, event | category | flops | bytes accessed | tf_op | source)
XLA Modules:
  0.0 115.6 jit_solution(14424761520104570861)
XLA Ops:
  0.6 0.0 copy-start
  0.6 0.0 copy-start.10
  0.7 0.0 copy-start.11
  0.7 4.2 %send.1 = f32[192,16,128]{2,1,0:T(8,128)} custom-call(s32[1]{0:T(128)} %bitcast.3.first_ref, s32[24,128]{1,0:T(8,128)} %bitcast.39, f32[48,128,128]{2,1,0:T(8,128)} %bitcast.33), custom_call_target="tpu_custom_call" | custom-call | tf_op jit(solution)/shard_map/send/pallas_call | solution.py:182
  4.9 5.8 %all-to-all-start = ((f32[192,16,128]{2,1,0:T(8,128)}), f32[192,16,128]{2,1,0:T(8,128)}, u32[]{:S(2)}, u32[]{:S(2)}) async-start(f32[192,16,128]{2,1,0:T(8,128)} %send.1), calls=%async_computation | async-start | bytes 3145728 | tf_op jit(solution)/shard_map/all_to_all | solution.py:197
  10.7 0.8 fusion.43
  11.5 0.3 convert_reduce_fusion
  11.7 0.6 subtract_select_fusion
  12.3 0.0 copy-done.10
  12.3 0.7 select_reduce_fusion
  13.2 0.1 stack.7
  13.2 0.0 copy-done.5
  13.2 1.7 %multiply_reduce_fusion = f32[512]{0:T(512)S(1)} fusion(f32[512]{0:T(512)S(1)} %copy-done.11, f32[3072]{0:T(1024)S(1)} %copy-done.4, f32[3072]{0:T(1024)S(1)} %copy-done.5), kind=kLoop, calls=%fused_computation.3 | loop fusion | flops 6290944 | bytes 28672 | tf_op jit(solution)/shard_map/reduce_sum | solution.py:246
  14.9 0.1 rsqrt.15
  15.0 2.1 %fusion.4 = (f32[384]{0:T(512)S(1)}, f32[384]{0:T(512)S(1)}, f32[384]{0:T(512)S(1)}, f32[384]{0:T(512)S(1)}) fusion(f32[3072]{0:T(1024)S(1)} %copy-done.4, s32[3072]{0:T(1024)S(1)} %copy-done.3, s32[384]{0:T(512)S(1)} %get-tuple-element.29, s32[384]{0:T(512)S(1)} %get-tuple-element.19, f32[3072]{0:T(1024)S(1)} %copy-done.5), kind=kLoop, calls=%fused_computation.10 | loop fusion | flops 11794944 | bytes 46080 | tf_op jit(solution)/shard_map/reduce_sum | solution.py:147
  17.2 0.1 mul.98
  17.3 0.1 sub.108
  17.4 0.0 copy-done
  17.4 3.4 %fusion.6 = f32[256,2048]{1,0:T(8,128)} fusion(f32[384,2048]{1,0:T(8,128)S(1)} %copy-done, f32[256]{0:T(256)S(1)} %mul.98, f32[256]{0:T(256)S(1)} %sub.108, f32[384]{0:T(512)S(1)} %get-tuple-element.11, f32[384]{0:T(512)S(1)} %get-tuple-element.12, f32[384]{0:T(512)S(1)} %get-tuple-element.26.sin_ref, f32[384]{0:T(512)S(1)} %get-tuple-element.10, ...), kind=kOutput, calls=%fused_computation.22 | convolution fusion | flops 1208745984 | bytes 5254144 | tf_op jit(solution)/shard_map/dot_general | solution.py:258
  20.8 0.0 collective-permute-start
  20.8 0.7 fusion.2
  21.6 0.3 convert_reduce_fusion.1
  21.9 0.8 select_reduce_fusion.1.source_ref
  22.7 8.7 %all-to-all-done.mates_hbm = f32[192,16,128]{2,1,0:T(8,128)} async-done(((f32[192,16,128]{2,1,0:T(8,128)}), f32[192,16,128]{2,1,0:T(8,128)}, u32[]{:S(2)}, u32[]{:S(2)}) %all-to-all-start) | async-done | bytes 1572896 | tf_op jit(solution)/shard_map/all_to_all | solution.py:197
  31.4 0.0 copy-done.6
  31.4 5.9 %rotate_pack.1 = f32[512,16,128]{2,1,0:T(8,128)} custom-call(s32[512]{0:T(512)} %select_reduce_fusion.1.source_ref, s32[384]{0:T(512)} %get-tuple-element.28.mate_ref, f32[384]{0:T(512)} %copy-done.8, f32[384]{0:T(512)} %copy-done.6, f32[48,128,128]{2,1,0:T(8,128)} %bitcast.34, f32[192,16,128]{2,1,0:T(8,128)} %all-to-all-done.mates_hbm), custom_call_target="tpu_custom_call" | custom-call | tf_op jit(solution)/shard_map/rotate_pack/pallas_call | solution.py:225
  37.2 0.0 copy-start.1
  37.3 9.6 %all-to-all-start.1 = ((f32[128,64,128]{2,1,0:T(8,128)}), f32[128,64,128]{2,1,0:T(8,128)}, u32[]{:S(2)}, u32[]{:S(2)}) async-start(f32[128,64,128]{2,1,0:T(8,128)} %bitcast.35), calls=%async_computation.1 | async-start | bytes 8388608 | tf_op jit(solution)/shard_map/all_to_all | solution.py:240
  46.8 0.1 mul.93
  46.9 0.1 sub.101
  47.0 0.0 collective-permute-done
  47.0 3.8 %convolution_add_fusion = f32[256,2048]{1,0:T(8,128)S(1)} fusion(f32[256,2048]{1,0:T(8,128)} %collective-permute-done, f32[384,2048]{1,0:T(8,128)S(1)} %copy-done.1, f32[256]{0:T(256)S(1)} %mul.93, f32[384]{0:T(512)S(1)} %get-tuple-element.11, f32[384]{0:T(512)S(1)} %get-tuple-element.12, f32[384]{0:T(512)S(1)} %copy-done.7, f32[256]{0:T(256)S(1)} %sub.101, ...), kind=kOutput, calls=%fused_computation.13 | convolution fusion | flops 1209270272 | bytes 7351296 | tf_op jit(solution)/shard_map/dot_general | solution.py:258
  50.8 0.1 slice_bitcast_fusion.2
  50.9 2.6 %collective-permute-start.3 = (f32[32,2048]{1,0:T(8,128)S(1)}, f32[32,2048]{1,0:T(8,128)S(1)}, u32[]{:S(2)}, u32[]{:S(2)}) collective-permute-start(f32[32,2048]{1,0:T(8,128)S(1)} %get-tuple-element.21), channel_id=1, source_target_pairs={{0,6},{1,7},{2,0},{3,1},{4,2},{5,3},{6,4},{7,5},{8,14},{9,15},{10,... | collective-permute-start | bytes 786440 | tf_op jit(solution)/shard_map/ppermute | solution.py:267
  53.5 0.0 collective-permute-start.1
  53.5 44.9 %collective-permute-done.3 = f32[32,2048]{1,0:T(8,128)S(1)} collective-permute-done((f32[32,2048]{1,0:T(8,128)S(1)}, f32[32,2048]{1,0:T(8,128)S(1)}, u32[]{:S(2)}, u32[]{:S(2)}) %collective-permute-start.3) | collective-permute-done | bytes 262176 | tf_op jit(solution)/shard_map/ppermute | solution.py:267
  98.4 1.2 %collective-permute-done.1 = f32[32,2048]{1,0:T(8,128)S(1)} collective-permute-done((f32[32,2048]{1,0:T(8,128)S(1)}, f32[32,2048]{1,0:T(8,128)S(1)}, u32[]{:S(2)}, u32[]{:S(2)}) %collective-permute-start.1) | collective-permute-done | bytes 262176 | tf_op jit(solution)/shard_map/ppermute | solution.py:267
  99.6 0.1 fusion.23
  99.7 0.1 collective-permute-start.2
  99.9 2.7 %collective-permute-start.4 = (f32[64,2048]{1,0:T(8,128)S(1)}, f32[64,2048]{1,0:T(8,128)S(1)}, u32[]{:S(2)}, u32[]{:S(2)}) collective-permute-start(f32[64,2048]{1,0:T(8,128)S(1)} %pad_maximum_fusion.1), channel_id=1, source_target_pairs={{0,6},{1,7},{2,0},{3,1},{4,2},{5,3},{6,4},{7,5},{8,14},{9,15},{10,... | collective-permute-start | bytes 1572872 | tf_op jit(solution)/shard_map/ppermute | solution.py:267
  102.6 0.1 and_select_fusion
  102.7 0.2 convert_reduce_fusion.2
  102.9 0.6 multiply_add_fusion.1.start_ref
  103.5 0.0 all-to-all-done.1
  103.5 4.6 %unpack.1 = f32[3,16,128,128]{3,2,1,0:T(8,128)} custom-call(s32[24]{0:T(128)} %multiply_add_fusion.1.start_ref, f32[512,16,128]{2,1,0:T(8,128)} %bitcast.8.in_ref), custom_call_target="tpu_custom_call" | custom-call | tf_op jit(solution)/shard_map/unpack/pallas_call | solution.py:292
  108.1 5.6 %collective-permute-done.2 = f32[64,2048]{1,0:T(8,128)S(1)} collective-permute-done((f32[64,2048]{1,0:T(8,128)S(1)}, f32[64,2048]{1,0:T(8,128)S(1)}, u32[]{:S(2)}, u32[]{:S(2)}) %collective-permute-start.2) | collective-permute-done | bytes 524320 | tf_op jit(solution)/shard_map/ppermute | solution.py:267
  113.6 0.0 collective-permute-done.4
  113.6 1.9 %fusion.5 = f32[64,2048]{1,0:T(8,128)} fusion(f32[64,2048]{1,0:T(8,128)S(1)} %collective-permute-done.4, f32[64,2048]{1,0:T(8,128)S(1)} %collective-permute-done.2, f32[256,2048]{1,0:T(8,128)} %copy-done.2), kind=kLoop, calls=%fused_computation.19 | loop fusion | flops 262144 | bytes 2097152 | tf_op jit(solution)/shard_map/add | solution.py:311
  (25 shorter events, 0.3 us)
Async XLA Ops:
  0.6 16.8 %copy-start = (f32[384,2048]{1,0:T(8,128)S(1)}, f32[384,2048]{1,0:T(8,128)}, u32[]{:S(2)}) copy-start(f32[384,2048]{1,0:T(8,128)} %param.7) | copy-start | bytes 9437188
  0.6 11.7 %copy-start.10 = (f32[3072]{0:T(1024)S(1)}, f32[3072]{0:T(1024)}, u32[]{:S(2)}) copy-start(f32[3072]{0:T(1024)} %param.9) | copy-start | bytes 36868
  0.7 12.5 %copy-start.11 = (f32[512]{0:T(512)S(1)}, f32[512]{0:T(512)}, u32[]{:S(2)}) copy-start(f32[512]{0:T(512)} %param.13) | copy-start | bytes 6148
  0.7 12.6 %copy-start.4 = (f32[3072]{0:T(1024)S(1)}, f32[3072]{0:T(1024)}, u32[]{:S(2)}) copy-start(f32[3072]{0:T(1024)} %param.11) | copy-start | bytes 36868
  0.7 12.6 %copy-start.5 = (f32[3072]{0:T(1024)S(1)}, f32[3072]{0:T(1024)}, u32[]{:S(2)}) copy-start(f32[3072]{0:T(1024)} %param.12) | copy-start | bytes 36868
  0.7 14.3 %copy-start.3 = (s32[3072]{0:T(1024)S(1)}, s32[3072]{0:T(1024)}, u32[]{:S(2)}) copy-start(s32[3072]{0:T(1024)} %param.10) | copy-start | bytes 36868
  4.9 26.5 %all-to-all-start = ((f32[192,16,128]{2,1,0:T(8,128)}), f32[192,16,128]{2,1,0:T(8,128)}, u32[]{:S(2)}, u32[]{:S(2)}) async-start(f32[192,16,128]{2,1,0:T(8,128)} %send.1), calls=%async_computation | async-start | bytes 3145728 | tf_op jit(solution)/shard_map/all_to_all | solution.py:197
  13.1 18.2 %copy-start.6 = (f32[384]{0:T(512)}, f32[384]{0:T(512)S(1)}, u32[]{:S(2)}) copy-start(f32[384]{0:T(512)S(1)} %get-tuple-element.26.sin_ref) | copy-start | bytes 4612
  13.1 18.2 %copy-start.8 = (f32[384]{0:T(512)}, f32[384]{0:T(512)S(1)}, u32[]{:S(2)}) copy-start(f32[384]{0:T(512)S(1)} %get-tuple-element.27.cos_ref) | copy-start | bytes 4612
  20.8 26.2 %collective-permute-start = (f32[256,2048]{1,0:T(8,128)}, f32[256,2048]{1,0:T(8,128)}, u32[]{:S(2)}, u32[]{:S(2)}) collective-permute-start(f32[256,2048]{1,0:T(8,128)} %fusion.6), channel_id=1, source_target_pairs={{0,1},{1,0},{2,3},{3,2},{4,5},{5,4},{6,7},{7,6},{8,9},{9,8},{10,11... | collective-permute-start | bytes 6291464 | tf_op jit(solution)/shard_map/ppermute | solution.py:271
  37.2 9.8 %copy-start.1 = (f32[384,2048]{1,0:T(8,128)S(1)}, f32[384,2048]{1,0:T(8,128)}, u32[]{:S(2)}) copy-start(f32[384,2048]{1,0:T(8,128)} %param.7) | copy-start | bytes 9437188
  37.2 9.8 %copy-start.7 = (f32[384]{0:T(512)S(1)}, f32[384]{0:T(512)}, u32[]{:S(2)}) copy-start(f32[384]{0:T(512)} %copy-done.6) | copy-start | bytes 4612
  37.3 9.8 %copy-start.9 = (f32[384]{0:T(512)S(1)}, f32[384]{0:T(512)}, u32[]{:S(2)}) copy-start(f32[384]{0:T(512)} %copy-done.8) | copy-start | bytes 4612
  37.3 66.2 %all-to-all-start.1 = ((f32[128,64,128]{2,1,0:T(8,128)}), f32[128,64,128]{2,1,0:T(8,128)}, u32[]{:S(2)}, u32[]{:S(2)}) async-start(f32[128,64,128]{2,1,0:T(8,128)} %bitcast.35), calls=%async_computation.1 | async-start | bytes 8388608 | tf_op jit(solution)/shard_map/all_to_all | solution.py:240
  50.8 48.8 %copy-start.2 = (f32[256,2048]{1,0:T(8,128)}, f32[256,2048]{1,0:T(8,128)S(1)}, u32[]{:S(2)}) copy-start(f32[256,2048]{1,0:T(8,128)S(1)} %convolution_add_fusion) | copy-start | bytes 6291460
  50.9 47.5 %collective-permute-start.3 = (f32[32,2048]{1,0:T(8,128)S(1)}, f32[32,2048]{1,0:T(8,128)S(1)}, u32[]{:S(2)}, u32[]{:S(2)}) collective-permute-start(f32[32,2048]{1,0:T(8,128)S(1)} %get-tuple-element.21), channel_id=1, source_target_pairs={{0,6},{1,7},{2,0},{3,1},{4,2},{5,3},{6,4},{7,5},{8,14},{9,15},{10,... | collective-permute-start | bytes 786440 | tf_op jit(solution)/shard_map/ppermute | solution.py:267
  53.5 46.1 %collective-permute-start.1 = (f32[32,2048]{1,0:T(8,128)S(1)}, f32[32,2048]{1,0:T(8,128)S(1)}, u32[]{:S(2)}, u32[]{:S(2)}) collective-permute-start(f32[32,2048]{1,0:T(8,128)S(1)} %get-tuple-element.23), channel_id=1, source_target_pairs={{0,2},{1,3},{2,4},{3,5},{4,6},{5,7},{6,0},{7,1},{8,10},{9,11},{10,... | collective-permute-start | bytes 786440 | tf_op jit(solution)/shard_map/ppermute | solution.py:267
  99.7 13.9 %collective-permute-start.2 = (f32[64,2048]{1,0:T(8,128)S(1)}, f32[64,2048]{1,0:T(8,128)S(1)}, u32[]{:S(2)}, u32[]{:S(2)}) collective-permute-start(f32[64,2048]{1,0:T(8,128)S(1)} %pad_maximum_fusion), channel_id=1, source_target_pairs={{0,2},{1,3},{2,4},{3,5},{4,6},{5,7},{6,0},{7,1},{8,10},{9,11},{10,... | collective-permute-start | bytes 1572872 | tf_op jit(solution)/shard_map/ppermute | solution.py:267
  99.9 13.8 %collective-permute-start.4 = (f32[64,2048]{1,0:T(8,128)S(1)}, f32[64,2048]{1,0:T(8,128)S(1)}, u32[]{:S(2)}, u32[]{:S(2)}) collective-permute-start(f32[64,2048]{1,0:T(8,128)S(1)} %pad_maximum_fusion.1), channel_id=1, source_target_pairs={{0,6},{1,7},{2,0},{3,1},{4,2},{5,3},{6,4},{7,5},{8,14},{9,15},{10,... | collective-permute-start | bytes 1572872 | tf_op jit(solution)/shard_map/ppermute | solution.py:267

commit v3 on v2

--- a/solution.py
+++ b/solution.py
@@ -24,7 +24,7 @@
     return rows.transpose(0, 2, 1, 3).reshape(count, width)
 
 
-def send_kernel(pair_cap, pieces, first_ref, mates_hbm, tiles_hbm, out_hbm,
+def send_kernel(pair_cap, pieces, mates_hbm, tiles_hbm, out_hbm,
                 mates_ref, tiles_ref, stage_ref, slots_ref, source_ref, sems):
     table = pltpu.make_async_copy(mates_hbm, mates_ref, sems.at[1])
     table.start()
@@ -35,7 +35,7 @@
     count = stage_ref.shape[0]
     blocks = count // pair_cap
     local = columns // LANES
-    local_mates = mates_ref[pl.ds(first_ref[0] * local, local), :]
+    local_mates = mates_ref[pl.ds(lax.axis_index("col") * local, local), :]
     owner = jnp.concatenate([local_mates[i : i + 1] for i in range(local)], axis=1) // columns
     member = lax.broadcasted_iota(jnp.int32, (blocks, columns), 0) == owner
     earlier = lax.broadcasted_iota(jnp.int32, (columns, columns), 0) < lax.broadcasted_iota(
@@ -88,8 +88,139 @@
         store.wait()
 
 
-def pack_kernel(pieces, source_ref, mate_ref, cos_ref, sin_ref, tiles_hbm, mates_hbm, out_hbm,
-                tiles_ref, rows_ref, stage_ref, load_sems, store_sems):
+def split(value, parts):
+    out = []
+    for _ in range(parts):
+        out.append(value.astype(jnp.bfloat16))
+        value = value - out[-1].astype(jnp.float32)
+    return out
+
+
+def panel_kernel(first_ref, mates_ref, theta_ref, kept_ref, pole_ref, weight_ref, zeros_ref, vec_hbm,
+                 spot_ref, cos_ref, sin_ref, theirs_hbm, ours_hbm,
+                 vec_ref, high_ref, low_ref, wide_high, wide_low, w_high, w_low,
+                 theirs_ref, ours_ref, load_sems, store_sems):
+    chunks = load_sems.shape[0]
+    columns, width = vec_ref.shape
+    step = width // chunks
+    loads = [
+        pltpu.make_async_copy(
+            vec_hbm.at[:, pl.ds(n * step, step)], vec_ref.at[:, pl.ds(n * step, step)],
+            load_sems.at[n],
+        )
+        for n in range(chunks)
+    ]
+    for load in loads:
+        load.start()
+
+    total, groups, local = kept_ref.shape[1], mates_ref.shape[0], columns // LANES
+    kept = kept_ref[...]
+    row_hot = lax.broadcasted_iota(jnp.int32, (groups, total), 0) == kept // LANES
+    lane_hot = (
+        lax.broadcasted_iota(jnp.int32, (LANES, total), 0) == kept % LANES
+    ).astype(jnp.bfloat16)
+    place = lax.broadcasted_iota(jnp.int32, (1, total), 1)
+    values = [(place // LANES).astype(jnp.float32), (place % LANES).astype(jnp.float32)]
+    for ref in (pole_ref, weight_ref):
+        values += [part.astype(jnp.float32) for part in split(ref[...], 3)]
+    spread = jnp.concatenate([jnp.where(row_hot, value, 0.0) for value in values], axis=0)
+    tables = lax.dot_general(
+        spread.astype(jnp.bfloat16), lane_hot, (((1,), (1,)), ((), ())),
+        preferred_element_type=jnp.float32,
+    )
+    tables = [tables[n * groups : (n + 1) * groups] for n in range(len(values))]
+    tables += [part.astype(jnp.float32) for part in split(theta_ref[...], 3)]
+
+    first = first_ref[0]
+    mine = (
+        lax.broadcasted_iota(jnp.int32, (groups, LANES), 0) - first * local
+    )
+
+    def here(table):
+        rows = [
+            jnp.sum(jnp.where(mine == n, table, jnp.zeros((), table.dtype)), axis=0, keepdims=True)
+            for n in range(local)
+        ]
+        return jnp.concatenate(rows, axis=1)
+
+    mates = here(mates_ref[...])
+    labels = first * columns + lax.broadcasted_iota(jnp.int32, (1, columns), 1)
+    mate_lane = (
+        lax.broadcasted_iota(jnp.int32, (LANES, columns), 0) == mates % LANES
+    ).astype(jnp.bfloat16)
+    mate_row = lax.broadcasted_iota(jnp.int32, (groups, columns), 0) == mates // LANES
+    wanted = jnp.concatenate(tables[2:], axis=0).astype(jnp.bfloat16)
+    picked = jnp.dot(wanted, mate_lane, preferred_element_type=jnp.float32)
+    theirs = [
+        jnp.sum(
+            jnp.where(mate_row, picked[n * groups : (n + 1) * groups], 0.0), axis=0, keepdims=True
+        )
+        for n in range(9)
+    ]
+    mate_pole, mate_weight, mate_theta = [
+        theirs[n] + (theirs[n + 1] + theirs[n + 2]) for n in (0, 3, 6)
+    ]
+    spot_ref[...] = here(tables[0] * LANES + tables[1]).astype(jnp.int32)
+    pole = here(tables[2] + (tables[3] + tables[4]))
+    weight = here(tables[5] + (tables[6] + tables[7]))
+    angle = jnp.where(mates < labels, mate_theta, here(theta_ref[...]))
+    paired = mates != labels
+    cosine = jnp.where(paired, jnp.cos(angle), 1.0)
+    sine = jnp.where(paired, jnp.where(labels < mates, -1.0, 1.0) * jnp.sin(angle), 0.0)
+    cos_ref[...] = cosine
+    sin_ref[...] = sine
+
+    own_part, mate_part = cosine * weight, sine * mate_weight
+    for q in range(zeros_ref.shape[0]):
+        zeros = jnp.broadcast_to(zeros_ref[q : q + 1], (LANES, LANES)).T
+        for t in range(local):
+            at = slice(t * LANES, (t + 1) * LANES)
+            value = own_part[:, at] / (pole[:, at] - zeros) - mate_part[:, at] / (
+                mate_pole[:, at] - zeros
+            )
+            high, low = split(value, 2)
+            wide_high[q * LANES : (q + 1) * LANES, at] = high
+            wide_low[q * LANES : (q + 1) * LANES, at] = low
+
+    half = theirs_ref.shape[0]
+    block = half // 4
+    chip, core = first // 2, first % 2
+    count = half // block
+    for parity in range(2):
+        for distance in range(count):
+            owner = (chip + distance) % count * 2 + (1 - core if parity == 0 else core)
+            source = pl.ds(pl.multiple_of(owner * block, block), block)
+            target = slice(parity * half + distance * block, parity * half + (distance + 1) * block)
+            w_high[target, :] = wide_high[source, :]
+            w_low[target, :] = wide_low[source, :]
+
+    stores = []
+    for parity, (stage, out) in enumerate(((theirs_ref, theirs_hbm), (ours_ref, ours_hbm))):
+        rows = slice(parity * half, (parity + 1) * half)
+        for n in range(chunks):
+            at = slice(n * step, (n + 1) * step)
+            if parity == 0:
+                loads[n].wait()
+                high_ref[:, at], low_ref[:, at] = split(vec_ref[:, at], 2)
+            high, low = high_ref[:, at], low_ref[:, at]
+            stage[:, at] = (
+                jnp.dot(w_high[rows, :], high, preferred_element_type=jnp.float32)
+                + jnp.dot(w_high[rows, :], low, preferred_element_type=jnp.float32)
+                + jnp.dot(w_low[rows, :], high, preferred_element_type=jnp.float32)
+            )
+            part = pl.ds(n * step, step)
+            store = pltpu.make_async_copy(
+                stage.at[:, part], out.at[:, part], store_sems.at[parity * chunks + n]
+            )
+            store.start()
+            stores.append(store)
+    for store in stores:
+        store.wait()
+
+
+def pack_kernel(pieces, source_hbm, mate_hbm, cos_hbm, sin_hbm, tiles_hbm, mates_hbm, out_hbm,
+                source_ref, mate_ref, cos_ref, sin_ref, tiles_ref, rows_ref, stage_ref,
+                load_sems, store_sems):
     local_rows, parts = tiles_ref.shape[0] * SUB, rows_ref.shape[1] // SUB
     own_load = pltpu.make_async_copy(tiles_hbm, tiles_ref, load_sems.at[0])
     mate_load = pltpu.make_async_copy(
@@ -97,6 +228,14 @@
     )
     own_load.start()
     mate_load.start()
+    tables = [
+        pltpu.make_async_copy(table, ref, load_sems.at[2 + n])
+        for n, (table, ref) in enumerate((
+            (source_hbm, source_ref), (mate_hbm, mate_ref), (cos_hbm, cos_ref), (sin_hbm, sin_ref)
+        ))
+    ]
+    for table in tables:
+        table.start()
     own_load.wait()
 
     def spread(g, carry):
@@ -109,11 +248,15 @@
         return carry
 
     lax.fori_loop(0, tiles_ref.shape[0], spread, 0, unroll=2)
+    for table in tables:
+        table.wait()
     mate_load.wait()
 
     def group(g, carry):
-        sources = [source_ref[g * GROUP + n] for n in range(GROUP)]
-        values = [cos_ref[i] * rows_ref[i] + sin_ref[i] * rows_ref[mate_ref[i]] for i in sources]
+        sources = [source_ref[0, g * GROUP + n] for n in range(GROUP)]
+        values = [
+            cos_ref[0, i] * rows_ref[i] + sin_ref[0, i] * rows_ref[mate_ref[0, i]] for i in sources
+        ]
         for n, value in enumerate(values):
             stage_ref[g * GROUP + n] = value
         return carry
@@ -130,17 +273,39 @@
         store.wait()
 
 
-def unpack_kernel(wanted, per_step, start_ref, in_ref, out_ref):
-    slots = in_ref.shape[0] // per_step
-    parts = in_ref.shape[1] // SUB
-    for r in range(per_step):
-        for first in range(0, wanted, SUB):
-            values = [in_ref[start_ref[first + n] + r * slots] for n in range(SUB)]
-            for n, value in enumerate(values):
-                for part in range(parts):
-                    out_ref[first // SUB, r, pl.ds(part * SUB * SUB + n, SUB, SUB), :] = value[
-                        part * SUB : (part + 1) * SUB
-                    ]
+def unpack_kernel(start_hbm, in_hbm, out_hbm, start_ref, in_ref, out_ref,
+                  table_sem, load_sems, store_sems):
+    pieces = load_sems.shape[0]
+    rows, parts = in_ref.shape[0], in_ref.shape[2] // SUB
+    wanted, per = start_ref.shape[1], rows // pieces
+    table = pltpu.make_async_copy(start_hbm, start_ref, table_sem)
+    table.start()
+    loads, stores = [], []
+    for n in range(pieces):
+        part = pl.ds(n * per, per)
+        loads.append(pltpu.make_async_copy(in_hbm.at[part], in_ref.at[part], load_sems.at[n]))
+        stores.append(
+            pltpu.make_async_copy(out_ref.at[:, part], out_hbm.at[:, part], store_sems.at[n])
+        )
+        loads[n].start()
+    table.wait()
+    for n in range(pieces):
+        loads[n].wait()
+
+        def row(r, carry):
+            for first in range(0, wanted, SUB):
+                values = [in_ref[r, start_ref[0, first + k]] for k in range(SUB)]
+                for k, value in enumerate(values):
+                    for part in range(parts):
+                        out_ref[first // SUB, r, pl.ds(part * SUB * SUB + k, SUB, SUB), :] = value[
+                            part * SUB : (part + 1) * SUB
+                        ]
+            return carry
+
+        lax.fori_loop(n * per, (n + 1) * per, row, 0)
+        stores[n].start()
+    for store in stores:
+        store.wait()
 
 
 def one_hot_sum(match, values):
@@ -168,11 +333,9 @@
     every = total_cols // dest_count
     move_cap = every // col_count + every // col_count // 3
     col_index = lax.axis_index("col")
-    chip, core = col_index // 2, col_index % 2
     first_col = col_index * block_cols
 
     order = jnp.arange(block_cols, dtype=jnp.int32)
-    labels = first_col + order
     mates = lax.dynamic_slice_in_dim(rotation_mate, first_col, block_cols)
     owner = mates // block_cols
     same_owner = owner[:, None] == owner[None, :]
@@ -182,7 +345,7 @@
     outgoing = pl.pallas_call(
         functools.partial(send_kernel, pair_cap, pieces),
         out_shape=jax.ShapeDtypeStruct((slot_count, lane_tiles, LANES), jnp.float32),
-        in_specs=[pl.BlockSpec(memory_space=pltpu.SMEM)] + [pl.BlockSpec(memory_space=pl.ANY)] * 2,
+        in_specs=[pl.BlockSpec(memory_space=pl.ANY)] * 2,
         out_specs=pl.BlockSpec(memory_space=pl.ANY),
         scratch_shapes=[
             pltpu.VMEM((total_cols // LANES, LANES), jnp.int32),
@@ -193,23 +356,50 @@
             pltpu.SemaphoreType.DMA((2 + pieces,)),
         ],
         name="send",
-    )(col_index[None], rotation_mate.reshape(-1, LANES), tiles)
+    )(rotation_mate.reshape(-1, LANES), tiles)
     incoming = lax.all_to_all(outgoing, "col", split_axis=0, concat_axis=0, tiled=True)
 
-    paired = mates != labels
-    own_match = kept_vectors[None, :] == labels[:, None]
-    mate_match = kept_vectors[None, :] == mates[:, None]
-    positions = jnp.arange(total_cols, dtype=jnp.int32)
-    spot = one_hot_sum(own_match, positions)
-    pole = one_hot_sum(own_match, secular_singularities)
-    weight = one_hot_sum(own_match, secular_coefficients)
-    mate_pole = one_hot_sum(mate_match, secular_singularities)
-    mate_weight = one_hot_sum(mate_match, secular_coefficients)
-    angle = one_hot_sum(positions[None, :] == jnp.minimum(labels, mates)[:, None], givens_theta)
-    sign_flip = jnp.where(labels < mates, -1.0, 1.0).astype(jnp.float32)
-    cosine = jnp.where(paired, jnp.cos(angle), 1.0)
-    sine = jnp.where(paired, sign_flip * jnp.sin(angle), 0.0)
-
+    half_cols = panel_cols // 2
+    vec_chunks = 4
+    spot, cosine, sine, theirs, ours = pl.pallas_call(
+        panel_kernel,
+        out_shape=[
+            jax.ShapeDtypeStruct((1, block_cols), jnp.int32),
+            jax.ShapeDtypeStruct((1, block_cols), jnp.float32),
+            jax.ShapeDtypeStruct((1, block_cols), jnp.float32),
+            jax.ShapeDtypeStruct((half_cols, block_rows), jnp.float32),
+            jax.ShapeDtypeStruct((half_cols, block_rows), jnp.float32),
+        ],
+        in_specs=[pl.BlockSpec(memory_space=pltpu.SMEM)]
+        + [pl.BlockSpec(memory_space=pltpu.VMEM)] * 6
+        + [pl.BlockSpec(memory_space=pl.ANY)],
+        out_specs=[pl.BlockSpec(memory_space=pltpu.VMEM)] * 3
+        + [pl.BlockSpec(memory_space=pl.ANY)] * 2,
+        scratch_shapes=[
+            pltpu.VMEM((block_cols, block_rows), jnp.float32),
+            pltpu.VMEM((block_cols, block_rows), jnp.bfloat16),
+            pltpu.VMEM((block_cols, block_rows), jnp.bfloat16),
+            pltpu.VMEM((panel_cols, block_cols), jnp.bfloat16),
+            pltpu.VMEM((panel_cols, block_cols), jnp.bfloat16),
+            pltpu.VMEM((panel_cols, block_cols), jnp.bfloat16),
+            pltpu.VMEM((panel_cols, block_cols), jnp.bfloat16),
+            pltpu.VMEM((half_cols, block_rows), jnp.float32),
+            pltpu.VMEM((half_cols, block_rows), jnp.float32),
+            pltpu.SemaphoreType.DMA((vec_chunks,)),
+            pltpu.SemaphoreType.DMA((2 * vec_chunks,)),
+        ],
+        name="panel",
+    )(
+        col_index[None],
+        rotation_mate.reshape(-1, LANES),
+        givens_theta.reshape(-1, LANES),
+        kept_vectors[None, :],
+        secular_singularities[None, :],
+        secular_coefficients[None, :],
+        secular_zeros.reshape(-1, LANES),
+        eigvec_halves,
+    )
+    spot = spot[0]
     recv_rank = jnp.sum((same_owner & (mates[None, :] < mates[:, None])).astype(jnp.int32), axis=1)
     remote = owner != col_index
     mate_row = jnp.where(remote, block_cols + owner * pair_cap + recv_rank, mates - first_col)
@@ -225,40 +415,31 @@
     parcels = pl.pallas_call(
         functools.partial(pack_kernel, pieces),
         out_shape=jax.ShapeDtypeStruct((places, lane_tiles, LANES), jnp.float32),
-        in_specs=[pl.BlockSpec(memory_space=pltpu.SMEM)] * 4
-        + [pl.BlockSpec(memory_space=pl.ANY)] * 2,
+        in_specs=[pl.BlockSpec(memory_space=pl.ANY)] * 6,
         out_specs=pl.BlockSpec(memory_space=pl.ANY),
         scratch_shapes=[
+            pltpu.SMEM((1, places), jnp.int32),
+            pltpu.SMEM((1, block_cols), jnp.int32),
+            pltpu.SMEM((1, block_cols), jnp.float32),
+            pltpu.SMEM((1, block_cols), jnp.float32),
             pltpu.VMEM(tiles.shape, jnp.float32),
             pltpu.VMEM((block_cols + slot_count, lane_tiles, LANES), jnp.float32),
             pltpu.VMEM((places, lane_tiles, LANES), jnp.float32),
-            pltpu.SemaphoreType.DMA((2,)),
+            pltpu.SemaphoreType.DMA((6,)),
             pltpu.SemaphoreType.DMA((pieces,)),
         ],
+        compiler_params=pltpu.CompilerParams(vmem_limit_bytes=50 * 1024 * 1024),
         name="rotate_pack",
-    )(place_source, mate_row, cosine, sine, tiles, incoming)
+    )(place_source[None, :], mate_row[None, :], cosine, sine, tiles, incoming)
     arrived = lax.all_to_all(
         parcels.reshape(dest_count, move_cap * lane_tiles, LANES),
         ("row", "col"), split_axis=0, concat_axis=0, tiled=True,
     )
 
-    raw = secular_coefficients[:, None] / (secular_singularities[:, None] - secular_zeros[None, :])
-    scale_all = lax.rsqrt(jnp.sum(raw * raw, axis=0) + 1e-06)
-    by_chip = jnp.stack([secular_zeros, scale_all]).reshape(2, chips, 2, panel_cols // col_count)
-    by_chip = jnp.concatenate([by_chip, by_chip], axis=1)
-    by_chip = lax.dynamic_slice_in_dim(by_chip, chip, chips, axis=1)
-
-    def partial_panel(parity):
-        mine = lax.dynamic_slice_in_dim(by_chip, parity, 1, axis=2).reshape(2, panel_cols // 2)
-        zeros, scale = mine[0], mine[1]
-        spun = (
-            cosine[:, None] * (weight[:, None] / (pole[:, None] - zeros[None, :]))
-            - sine[:, None] * (mate_weight[:, None] / (mate_pole[:, None] - zeros[None, :]))
-        ) * scale[None, :]
-        return lax.dot_general(
-            spun, eigvec_halves, (((0,), (0,)), ((), ())),
-            precision=lax.Precision.HIGH, preferred_element_type=jnp.float32,
-        )
+    share = panel_cols // col_count
+    zeros_here = lax.dynamic_slice_in_dim(secular_zeros, col_index * share, share)
+    raw = secular_coefficients[:, None] / (secular_singularities[:, None] - zeros_here[None, :])
+    scale = lax.rsqrt(jnp.sum(raw * raw, axis=0) + 1e-06)
 
     def shift(array, chip_step):
         pairs = [
@@ -267,14 +448,19 @@
         return lax.ppermute(array, "col", pairs)
 
     swap = [(c, c ^ 1) for c in range(col_count)]
-    theirs = partial_panel(1 - core)
     partner = lax.ppermute(theirs, "col", swap)
-    both = (partial_panel(core) + partner).reshape(chips, panel_cols // col_count, block_rows)
-    half = panel_cols // col_count // 2
-    far_up = shift(both[2, :half], 1)
-    far_down = shift(both[2, half:], -1)
-    up = shift(jnp.concatenate([both[1, :half] + far_up, both[1, half:]]), 1)
-    down = shift(jnp.concatenate([both[3, :half], both[3, half:] + far_down]), -1)
+    ours = ours.reshape(chips, share, block_rows)
+    partner = partner.reshape(chips, share, block_rows)
+    half = share // 2
+
+    def pair(distance, rows):
+        return ours[distance, rows] + partner[distance, rows]
+
+    low, high = slice(0, half), slice(half, share)
+    up = shift(jnp.concatenate([pair(2, low), pair(1, high)]), 1)
+    down = shift(jnp.concatenate([pair(2, high), pair(3, low)]), -1)
+    up_low = shift(pair(1, low) + up[:half], 1)
+    down_high = shift(pair(3, high) + down[:half], -1)
 
     slot_index = lax.axis_index("row") * col_count + col_index
     wanted = lax.dynamic_slice_in_dim(kept_vectors, slot_index * every, every)
@@ -287,28 +473,28 @@
         axis=1,
     )
     starts = source * move_cap + source_rank
-    steps = 4
-    per_step = row_count // steps
     packed = pl.pallas_call(
-        functools.partial(unpack_kernel, every, per_step),
-        grid=(steps,),
+        unpack_kernel,
         out_shape=jax.ShapeDtypeStruct(
             (every // SUB, row_count, lane_tiles * SUB, LANES), jnp.float32
         ),
-        in_specs=[
-            pl.BlockSpec(memory_space=pltpu.SMEM),
-            pl.BlockSpec(
-                (per_step * col_count * move_cap, lane_tiles, LANES), lambda s: (s, 0, 0)
-            ),
+        in_specs=[pl.BlockSpec(memory_space=pl.ANY)] * 2,
+        out_specs=pl.BlockSpec(memory_space=pl.ANY),
+        scratch_shapes=[
+            pltpu.SMEM((1, every), jnp.int32),
+            pltpu.VMEM((row_count, col_count * move_cap, lane_tiles, LANES), jnp.float32),
+            pltpu.VMEM((every // SUB, row_count, lane_tiles * SUB, LANES), jnp.float32),
+            pltpu.SemaphoreType.DMA,
+            pltpu.SemaphoreType.DMA((pieces,)),
+            pltpu.SemaphoreType.DMA((pieces,)),
         ],
-        out_specs=pl.BlockSpec(
-            (every // SUB, per_step, lane_tiles * SUB, LANES), lambda s: (0, s, 0, 0)
-        ),
         name="unpack",
-    )(starts, arrived.reshape(dest_count * move_cap, lane_tiles, LANES))
+    )(starts[None, :], arrived.reshape(row_count, col_count * move_cap, lane_tiles, LANES))
     packed_vectors = from_tiles(packed.reshape(-1, LANES), every, row_count * block_rows)
-    packed_vectors, up, down = lax.optimization_barrier((packed_vectors, up, down))
-    panel = both[0] + up + down
+    base = pair(0, slice(0, share)) + jnp.concatenate([down[half:], up[half:]])
+    base = lax.optimization_barrier(base * scale[:, None])
+    packed_vectors, up_low, down_high = lax.optimization_barrier((packed_vectors, up_low, down_high))
+    panel = base + jnp.concatenate([up_low, down_high]) * scale[:, None]
     return (packed_vectors, panel)
 
 

time: 116 us -> 118 us (1.017)
  matrix products: 7.23 us -> 0 us
  Pallas kernels: 14.6 us -> 21.5 us
  waiting for transfers between devices: 60.4 us -> 62.5 us
  local copies, waits for them, and re-layouts: 0.66 us -> 2.11 us
    pallas_call x1 -> x2, Pallas kernels: 4.59 us -> 12.3 us  [the longest x1 9 us: shards(): pl.pallas_call(panel_kernel, out_shape=[jax.ShapeDtypeStruct((1, block_co...]
    dot_general x2 -> x0, matrix products: 7.23 us -> none  [partial_panel(): lax.dot_general(spun, eigvec_halves, (((0,), (0,)), ((), ())), precision=...]
    reduce_sum x4 -> x1, other arithmetic: 4.39 us -> 0.16 us  [one_hot_sum(): jnp.sum(jnp.where(match, values[None, :], jnp.zeros((), values.dtype)), a...]
    add x3, other arithmetic: 2.58 us -> 4.35 us  [the longest x1 1.86 us: shards(): panel = base + jnp.concatenate([up_low, down_high]) * scale[:, None]]
    ppermute x4, waiting for transfers between devices: 51.7 us -> 53.2 us  [shift(): return lax.ppermute(array, 'col', pairs)]
    reduce_sum x1, other arithmetic: 1.67 us -> 0.31 us  [shards(): scale = lax.rsqrt(jnp.sum(raw * raw, axis=0) + 1e-06)]
    broadcast_in_dim x0 -> x1, other arithmetic: none -> 1.3 us  [shards(): starts[None, :]]
    unnamed x24 -> x10, local copies, waits for them, and re-layouts: 0.06 us -> 1.35 us
  transfers between devices with their start and end apart: 7 -> 7, of which waited for: 4 -> 4; matrix products, arithmetic and copies ran while one was open for 15% -> 8% of each run, Pallas kernels for 9% -> 15%
where the time goes in v3:
time: 118 us; the launch traced here: 117 us
  waiting for transfers between devices  62.5 us (53%)
  Pallas kernels  21.5 us (18%)
  starting transfers between devices  19.8 us (17%)
  other arithmetic  10.4 us (9%)
  local copies, waits for them, and re-layouts  2.11 us (2%)
    ppermute x4, waiting for transfers between devices, shift(): return lax.ppermute(array, 'col', pairs)  53.2 us
    all_to_all x1, starting transfers between devices, shards(): lax.all_to_all(parcels.reshape(dest_count, move_cap * lane_tiles, LANES),...  9.57 us
    all_to_all x1, waiting for transfers between devices, shards(): lax.all_to_all(outgoing, 'col', split_axis=0, concat_axis=0, tiled=True)  9.22 us
    pallas_call x1, Pallas kernels, shards(): pl.pallas_call(panel_kernel, out_shape=[jax.ShapeDtypeStruct((1, block_co...  9 us
    all_to_all x1, starting transfers between devices, shards(): lax.all_to_all(outgoing, 'col', split_axis=0, concat_axis=0, tiled=True)  5.8 us
    pallas_call x1, Pallas kernels, shards(): pl.pallas_call(functools.partial(pack_kernel, pieces), out_shape=jax.Shap...  5.14 us
    ppermute x4, starting transfers between devices, shift(): return lax.ppermute(array, 'col', pairs)  4.35 us
    pallas_call x1, Pallas kernels, shards(): pl.pallas_call(functools.partial(send_kernel, pair_cap, pieces), out_shap...  4.04 us
  transfers between devices with their start and end apart: 7, of which 4 were waited for; matrix products, arithmetic and copies ran while one was open for 8% of the time, Pallas kernels for 15%

profile of v3, /device:TPU:1, one launch (start us, length us, event | category | flops | bytes accessed | tf_op | source)
XLA Modules:
  0.0 117.1 jit_solution(15008537598345197502)
XLA Ops:
  0.6 4.0 %send.1 = f32[192,16,128]{2,1,0:T(8,128)} custom-call(s32[24,128]{1,0:T(8,128)} %bitcast.47, f32[48,128,128]{2,1,0:T(8,128)} %bitcast.41), custom_call_target="tpu_custom_call" | custom-call | tf_op jit(solution)/shard_map/send/pallas_call | solution.py:345
  4.7 5.8 %all-to-all-start = ((f32[192,16,128]{2,1,0:T(8,128)}), f32[192,16,128]{2,1,0:T(8,128)S(1)}, u32[]{:S(2)}, u32[]{:S(2)}) async-start(f32[192,16,128]{2,1,0:T(8,128)} %send.1), calls=%async_computation | async-start | bytes 3145728 | tf_op jit(solution)/shard_map/all_to_all | solution.py:360
  10.5 9.0 %panel.1 = (s32[1,384]{1,0:T(1,128)}, f32[1,384]{1,0:T(1,128)}, f32[1,384]{1,0:T(1,128)}, f32[256,2048]{1,0:T(8,128)}, f32[256,2048]{1,0:T(8,128)}) custom-call(s32[1]{0:T(128)} %bitcast.1.first_ref, s32[24,128]{1,0:T(8,128)} %bitcast.48, f32[24,128]{1,0:T(8,128)} %bitcast.52, s32[1,3072]{1,0:T(1,128)} %bitcast.51, f32[1,3072]{1,0:T(1,128)} %bitcast.49, ...), custom_call_target="tpu_custom_call" | custom-call | tf_op jit(solution)/shard_map/panel/pallas_call | solution.py:364
  19.5 0.1 collective-permute-start
  19.6 0.8 add_select_fusion
  20.4 0.3 convert_reduce_fusion
  20.6 0.7 fusion.12
  21.4 0.3 convert_reduce_fusion.1
  21.7 0.2 select_reduce_fusion
  21.8 9.2 %all-to-all-done.mates_hbm = f32[192,16,128]{2,1,0:T(8,128)S(1)} async-done(((f32[192,16,128]{2,1,0:T(8,128)}), f32[192,16,128]{2,1,0:T(8,128)S(1)}, u32[]{:S(2)}, u32[]{:S(2)}) %all-to-all-start) | async-done | bytes 1572896 | tf_op jit(solution)/shard_map/all_to_all | solution.py:360
  31.1 0.0 copy-start
  31.1 0.7 copy-done
  31.7 0.0 copy-start.1
  31.7 0.7 copy-done.1
  32.4 5.1 %rotate_pack.1 = f32[512,16,128]{2,1,0:T(8,128)} custom-call(s32[1,512]{1,0:T(1,128)S(1)} %bitcast.40, s32[1,384]{1,0:T(1,128)S(1)} %broadcast_in_dim.59.mate_hbm, f32[1,384]{1,0:T(1,128)S(1)} %copy-done, f32[1,384]{1,0:T(1,128)S(1)} %copy-done.1, f32[48,128,128]{2,1,0:T(8,128)} %bitcast.42, f32[192,16,128]{2,1,0:T(8,128)S(1)} %all-to-all-done.mates_hbm), custom_call_target="tpu_custom_call" | custom-call | tf_op jit(solution)/shard_map/rotate_pack/pallas_call | solution.py:415
  37.5 0.0 copy-start.3
  37.6 0.0 copy-start.4
  37.6 0.0 copy-start.2
  37.6 9.6 %all-to-all-start.1 = ((f32[128,64,128]{2,1,0:T(8,128)}), f32[128,64,128]{2,1,0:T(8,128)}, u32[]{:S(2)}, u32[]{:S(2)}) async-start(f32[128,64,128]{2,1,0:T(8,128)} %bitcast.43), calls=%async_computation.1 | async-start | bytes 8388608 | tf_op jit(solution)/shard_map/all_to_all | solution.py:434
  47.2 0.8 dynamic_slice.11
  47.9 0.8 and_select_fusion.1
  48.7 0.0 copy-done.3
  48.7 0.0 copy-done.4
  48.7 0.3 multiply_reduce_fusion
  49.0 0.0 collective-permute-done
  49.0 0.0 copy-done.2
  49.0 1.3 %fusion.4 = (f32[32,2048]{1,0:T(8,128)S(1)}, f32[32,2048]{1,0:T(8,128)S(1)}, f32[32,2048]{1,0:T(8,128)S(1)}, f32[32,2048]{1,0:T(8,128)S(1)}) fusion(f32[4,64,2048]{2,1,0:T(8,128)} %bitcast.20, f32[4,64,2048]{2,1,0:T(8,128)S(1)} %bitcast.45), kind=kLoop, calls=%fused_computation.16 | loop fusion | flops 262144 | bytes 3145728 | tf_op jit(solution)/shard_map/add | solution.py:457
  50.4 1.4 %collective-permute-start.1 = (f32[64,2048]{1,0:T(8,128)S(1)}, f32[64,2048]{1,0:T(8,128)S(1)}, u32[]{:S(2)}, u32[]{:S(2)}) collective-permute-start(f32[64,2048]{1,0:T(8,128)S(1)} %pad_maximum_fusion), channel_id=1, source_target_pairs={{0,2},{1,3},{2,4},{3,5},{4,6},{5,7},{6,0},{7,1},{8,10},{9,11},{10,... | collective-permute-start | bytes 1572872 | tf_op jit(solution)/shard_map/ppermute | solution.py:448
  51.9 1.4 %collective-permute-start.3 = (f32[64,2048]{1,0:T(8,128)S(1)}, f32[64,2048]{1,0:T(8,128)S(1)}, u32[]{:S(2)}, u32[]{:S(2)}) collective-permute-start(f32[64,2048]{1,0:T(8,128)S(1)} %pad_maximum_fusion.1), channel_id=1, source_target_pairs={{0,6},{1,7},{2,0},{3,1},{4,2},{5,3},{6,4},{7,5},{8,14},{9,15},{10,... | collective-permute-start | bytes 1572872 | tf_op jit(solution)/shard_map/ppermute | solution.py:448
  53.3 0.2 convert_reduce_fusion.2
  53.4 1.3 %add_bitcast_fusion.start_hbm = s32[1,24]{1,0:T(1,128)} fusion(s32[24]{0:T(128)S(1)} %convert_reduce_fusion.2, s32[3072]{0:T(1024)} %param.10, s32[]{:T(128)S(6)} %select_n.37), kind=kLoop, calls=%fused_computation.42 | loop fusion | flops 240 | bytes 292 | tf_op jit(solution)/shard_map/broadcast_in_dim | solution.py:492
  54.7 50.7 %collective-permute-done.1 = f32[64,2048]{1,0:T(8,128)S(1)} collective-permute-done((f32[64,2048]{1,0:T(8,128)S(1)}, f32[64,2048]{1,0:T(8,128)S(1)}, u32[]{:S(2)}, u32[]{:S(2)}) %collective-permute-start.1) | collective-permute-done | bytes 524320 | tf_op jit(solution)/shard_map/ppermute | solution.py:448
  105.5 0.0 collective-permute-done.3
  105.5 1.2 %slice_add_fusion.1 = (f32[32,2048]{1,0:T(8,128)S(1)}, f32[32,2048]{1,0:T(8,128)S(1)}, f32[32,2048]{1,0:T(8,128)S(1)}, f32[32,2048]{1,0:T(8,128)S(1)}) fusion(f32[64,2048]{1,0:T(8,128)S(1)} %collective-permute-done.3, f32[4,64,2048]{2,1,0:T(8,128)} %bitcast.20, f32[4,64,2048]{2,1,0:T(8,128)S(1)} %bitcast.46, f32[64,2048]{1,0:T(8,128)S(1)} %collective-permute-done.1), kind=kLoop, calls=%fused_computation.12 | loop fusion | flops 262144 | bytes 3145728 | tf_op jit(solution)/shard_map/add | solution.py:463
  106.6 0.6 collective-permute-start.4
  107.3 0.9 collective-permute-start.2
  108.2 1.2 %fusion.1 = f32[64,2048]{1,0:T(8,128)S(1)} fusion(f32[256,2048]{1,0:T(8,128)} %collective-permute-done, f32[32,2048]{1,0:T(8,128)S(1)} %get-tuple-element.28, f32[32,2048]{1,0:T(8,128)S(1)} %get-tuple-element.29, f32[256,2048]{1,0:T(8,128)S(1)} %copy-done.2, f32[64]{0:T(128)S(1)} %add_rsqrt_fusion), kind=kLoop, calls=%fused_computation.7 | loop fusion | flops 524288 | bytes 2097408 | tf_op jit(solution)/shard_map/mul | solution.py:495
  109.4 0.0 all-to-all-done.1
  109.4 3.3 %unpack.1 = f32[3,16,128,128]{3,2,1,0:T(8,128)} custom-call(s32[1,24]{1,0:T(1,128)} %add_bitcast_fusion.start_hbm, f32[16,32,16,128]{3,2,1,0:T(8,128)} %bitcast.15.in_hbm), custom_call_target="tpu_custom_call" | custom-call | tf_op jit(solution)/shard_map/unpack/pallas_call | solution.py:476
  112.7 1.0 collective-permute-done.4
  113.7 1.5 %collective-permute-done.2 = f32[32,2048]{1,0:T(8,128)} collective-permute-done((f32[32,2048]{1,0:T(8,128)S(1)}, f32[32,2048]{1,0:T(8,128)}, u32[]{:S(2)}, u32[]{:S(2)}) %collective-permute-start.2) | collective-permute-done | bytes 262176 | tf_op jit(solution)/shard_map/ppermute | solution.py:448
  115.2 1.9 %fusion.2 = f32[64,2048]{1,0:T(8,128)} fusion(f32[64,2048]{1,0:T(8,128)S(1)} %fusion.1, f32[32,2048]{1,0:T(8,128)S(1)} %collective-permute-done.4, f32[32,2048]{1,0:T(8,128)} %collective-permute-done.2, f32[64]{0:T(128)S(1)} %add_rsqrt_fusion), kind=kLoop, calls=%fused_computation.11 | loop fusion | flops 393216 | bytes 1573120 | tf_op jit(solution)/shard_map/add | solution.py:497
  (7 shorter events, 0.1 us)
Async XLA Ops:
  4.7 26.4 %all-to-all-start = ((f32[192,16,128]{2,1,0:T(8,128)}), f32[192,16,128]{2,1,0:T(8,128)S(1)}, u32[]{:S(2)}, u32[]{:S(2)}) async-start(f32[192,16,128]{2,1,0:T(8,128)} %send.1), calls=%async_computation | async-start | bytes 3145728 | tf_op jit(solution)/shard_map/all_to_all | solution.py:360
  19.5 29.6 %collective-permute-start = (f32[256,2048]{1,0:T(8,128)}, f32[256,2048]{1,0:T(8,128)}, u32[]{:S(2)}, u32[]{:S(2)}) collective-permute-start(f32[256,2048]{1,0:T(8,128)} %get-tuple-element.14), channel_id=1, source_target_pairs={{0,1},{1,0},{2,3},{3,2},{4,5},{5,4},{6,7},{7,6},{8,9},{9,8},{10,11... | collective-permute-start | bytes 6291464 | tf_op jit(solution)/shard_map/ppermute | solution.py:451
  31.1 0.7 copy-start
  31.7 0.7 copy-start.1
  37.5 11.2 %copy-start.3 = (f32[3072]{0:T(1024)S(1)}, f32[3072]{0:T(1024)}, u32[]{:S(2)}) copy-start(f32[3072]{0:T(1024)} %param.11) | copy-start | bytes 36868
  37.6 11.2 %copy-start.4 = (f32[3072]{0:T(1024)S(1)}, f32[3072]{0:T(1024)}, u32[]{:S(2)}) copy-start(f32[3072]{0:T(1024)} %param.12) | copy-start | bytes 36868
  37.6 11.5 %copy-start.2 = (f32[256,2048]{1,0:T(8,128)S(1)}, f32[256,2048]{1,0:T(8,128)}, u32[]{:S(2)}) copy-start(f32[256,2048]{1,0:T(8,128)} %get-tuple-element.13) | copy-start | bytes 6291460
  37.6 71.8 %all-to-all-start.1 = ((f32[128,64,128]{2,1,0:T(8,128)}), f32[128,64,128]{2,1,0:T(8,128)}, u32[]{:S(2)}, u32[]{:S(2)}) async-start(f32[128,64,128]{2,1,0:T(8,128)} %bitcast.43), calls=%async_computation.1 | async-start | bytes 8388608 | tf_op jit(solution)/shard_map/all_to_all | solution.py:434
  50.4 55.0 %collective-permute-start.1 = (f32[64,2048]{1,0:T(8,128)S(1)}, f32[64,2048]{1,0:T(8,128)S(1)}, u32[]{:S(2)}, u32[]{:S(2)}) collective-permute-start(f32[64,2048]{1,0:T(8,128)S(1)} %pad_maximum_fusion), channel_id=1, source_target_pairs={{0,2},{1,3},{2,4},{3,5},{4,6},{5,7},{6,0},{7,1},{8,10},{9,11},{10,... | collective-permute-start | bytes 1572872 | tf_op jit(solution)/shard_map/ppermute | solution.py:448
  51.9 53.6 %collective-permute-start.3 = (f32[64,2048]{1,0:T(8,128)S(1)}, f32[64,2048]{1,0:T(8,128)S(1)}, u32[]{:S(2)}, u32[]{:S(2)}) collective-permute-start(f32[64,2048]{1,0:T(8,128)S(1)} %pad_maximum_fusion.1), channel_id=1, source_target_pairs={{0,6},{1,7},{2,0},{3,1},{4,2},{5,3},{6,4},{7,5},{8,14},{9,15},{10,... | collective-permute-start | bytes 1572872 | tf_op jit(solution)/shard_map/ppermute | solution.py:448
  106.6 7.1 %collective-permute-start.4 = (f32[32,2048]{1,0:T(8,128)S(1)}, f32[32,2048]{1,0:T(8,128)S(1)}, u32[]{:S(2)}, u32[]{:S(2)}) collective-permute-start(f32[32,2048]{1,0:T(8,128)S(1)} %get-tuple-element.22), channel_id=1, source_target_pairs={{0,6},{1,7},{2,0},{3,1},{4,2},{5,3},{6,4},{7,5},{8,14},{9,15},{10,... | collective-permute-start | bytes 786440 | tf_op jit(solution)/shard_map/ppermute | solution.py:448
  107.3 7.9 %collective-permute-start.2 = (f32[32,2048]{1,0:T(8,128)S(1)}, f32[32,2048]{1,0:T(8,128)}, u32[]{:S(2)}, u32[]{:S(2)}) collective-permute-start(f32[32,2048]{1,0:T(8,128)S(1)} %get-tuple-element.23), channel_id=1, source_target_pairs={{0,2},{1,3},{2,4},{3,5},{4,6},{5,7},{6,0},{7,1},{8,10},{9,11},{10,... | collective-permute-start | bytes 786440 | tf_op jit(solution)/shard_map/ppermute | solution.py:448

commit v4 on v3

--- a/solution.py
+++ b/solution.py
@@ -96,9 +96,9 @@
     return out
 
 
-def panel_kernel(first_ref, mates_ref, theta_ref, kept_ref, pole_ref, weight_ref, zeros_ref, vec_hbm,
+def panel_kernel(mates_ref, theta_ref, kept_ref, pole_ref, weight_ref, zeros_ref, vec_hbm,
                  spot_ref, cos_ref, sin_ref, theirs_hbm, ours_hbm,
-                 vec_ref, high_ref, low_ref, wide_high, wide_low, w_high, w_low,
+                 vec_ref, deep_ref, wide_high, wide_low, w_ref,
                  theirs_ref, ours_ref, load_sems, store_sems):
     chunks = load_sems.shape[0]
     columns, width = vec_ref.shape
@@ -131,7 +131,7 @@
     tables = [tables[n * groups : (n + 1) * groups] for n in range(len(values))]
     tables += [part.astype(jnp.float32) for part in split(theta_ref[...], 3)]
 
-    first = first_ref[0]
+    first = lax.axis_index("col")
     mine = (
         lax.broadcasted_iota(jnp.int32, (groups, LANES), 0) - first * local
     )
@@ -191,8 +191,9 @@
             owner = (chip + distance) % count * 2 + (1 - core if parity == 0 else core)
             source = pl.ds(pl.multiple_of(owner * block, block), block)
             target = slice(parity * half + distance * block, parity * half + (distance + 1) * block)
-            w_high[target, :] = wide_high[source, :]
-            w_low[target, :] = wide_low[source, :]
+            w_ref[target, 0:columns] = wide_high[source, :]
+            w_ref[target, columns : 2 * columns] = wide_high[source, :]
+            w_ref[target, 2 * columns :] = wide_low[source, :]
 
     stores = []
     for parity, (stage, out) in enumerate(((theirs_ref, theirs_hbm), (ours_ref, ours_hbm))):
@@ -201,12 +202,12 @@
             at = slice(n * step, (n + 1) * step)
             if parity == 0:
                 loads[n].wait()
-                high_ref[:, at], low_ref[:, at] = split(vec_ref[:, at], 2)
-            high, low = high_ref[:, at], low_ref[:, at]
-            stage[:, at] = (
-                jnp.dot(w_high[rows, :], high, preferred_element_type=jnp.float32)
-                + jnp.dot(w_high[rows, :], low, preferred_element_type=jnp.float32)
-                + jnp.dot(w_low[rows, :], high, preferred_element_type=jnp.float32)
+                high, low = split(vec_ref[:, at], 2)
+                deep_ref[0:columns, at] = high
+                deep_ref[columns : 2 * columns, at] = low
+                deep_ref[2 * columns :, at] = high
+            stage[:, at] = jnp.dot(
+                w_ref[rows, :], deep_ref[:, at], preferred_element_type=jnp.float32
             )
             part = pl.ds(n * step, step)
             store = pltpu.make_async_copy(
@@ -218,25 +219,18 @@
         store.wait()
 
 
-def pack_kernel(pieces, source_hbm, mate_hbm, cos_hbm, sin_hbm, tiles_hbm, mates_hbm, out_hbm,
-                source_ref, mate_ref, cos_ref, sin_ref, tiles_ref, rows_ref, stage_ref,
-                load_sems, store_sems):
-    local_rows, parts = tiles_ref.shape[0] * SUB, rows_ref.shape[1] // SUB
-    own_load = pltpu.make_async_copy(tiles_hbm, tiles_ref, load_sems.at[0])
-    mate_load = pltpu.make_async_copy(
-        mates_hbm, rows_ref.at[pl.ds(local_rows, mates_hbm.shape[0])], load_sems.at[1]
-    )
-    own_load.start()
-    mate_load.start()
-    tables = [
-        pltpu.make_async_copy(table, ref, load_sems.at[2 + n])
-        for n, (table, ref) in enumerate((
-            (source_hbm, source_ref), (mate_hbm, mate_ref), (cos_hbm, cos_ref), (sin_hbm, sin_ref)
+def turn_kernel(mate_hbm, cos_hbm, sin_hbm, tiles_hbm, turned_ref,
+                mate_ref, cos_ref, sin_ref, tiles_ref, rows_ref, sems):
+    loads = [
+        pltpu.make_async_copy(source, ref, sems.at[n])
+        for n, (source, ref) in enumerate((
+            (tiles_hbm, tiles_ref), (mate_hbm, mate_ref), (cos_hbm, cos_ref), (sin_hbm, sin_ref)
         ))
     ]
-    for table in tables:
-        table.start()
-    own_load.wait()
+    for load in loads:
+        load.start()
+    loads[0].wait()
+    parts = rows_ref.shape[1] // SUB
 
     def spread(g, carry):
         values = [
@@ -248,15 +242,37 @@
         return carry
 
     lax.fori_loop(0, tiles_ref.shape[0], spread, 0, unroll=2)
+    for load in loads[1:]:
+        load.wait()
+
+    def turn(g, carry):
+        columns = [g * GROUP + n for n in range(GROUP)]
+        values = [
+            cos_ref[0, i] * rows_ref[i] + sin_ref[0, i] * rows_ref[mate_ref[0, i]] for i in columns
+        ]
+        for i, value in zip(columns, values):
+            turned_ref[i] = value
+        return carry
+
+    lax.fori_loop(0, rows_ref.shape[0] // GROUP, turn, 0, unroll=2)
+
+
+def pack_kernel(pieces, source_hbm, mate_hbm, sin_hbm, turned_ref, mates_ref, out_hbm,
+                source_ref, mate_ref, sin_ref, stage_ref, load_sems, store_sems):
+    tables = [
+        pltpu.make_async_copy(table, ref, load_sems.at[n])
+        for n, (table, ref) in enumerate(
+            ((source_hbm, source_ref), (mate_hbm, mate_ref), (sin_hbm, sin_ref))
+        )
+    ]
+    for table in tables:
+        table.start()
     for table in tables:
         table.wait()
-    mate_load.wait()
 
     def group(g, carry):
         sources = [source_ref[0, g * GROUP + n] for n in range(GROUP)]
-        values = [
-            cos_ref[0, i] * rows_ref[i] + sin_ref[0, i] * rows_ref[mate_ref[0, i]] for i in sources
-        ]
+        values = [turned_ref[i] + sin_ref[0, i] * mates_ref[mate_ref[0, i]] for i in sources]
         for n, value in enumerate(values):
             stage_ref[g * GROUP + n] = value
         return carry
@@ -360,7 +376,7 @@
     incoming = lax.all_to_all(outgoing, "col", split_axis=0, concat_axis=0, tiled=True)
 
     half_cols = panel_cols // 2
-    vec_chunks = 4
+    vec_chunks = 2
     spot, cosine, sine, theirs, ours = pl.pallas_call(
         panel_kernel,
         out_shape=[
@@ -370,19 +386,16 @@
             jax.ShapeDtypeStruct((half_cols, block_rows), jnp.float32),
             jax.ShapeDtypeStruct((half_cols, block_rows), jnp.float32),
         ],
-        in_specs=[pl.BlockSpec(memory_space=pltpu.SMEM)]
-        + [pl.BlockSpec(memory_space=pltpu.VMEM)] * 6
+        in_specs=[pl.BlockSpec(memory_space=pltpu.VMEM)] * 6
         + [pl.BlockSpec(memory_space=pl.ANY)],
         out_specs=[pl.BlockSpec(memory_space=pltpu.VMEM)] * 3
         + [pl.BlockSpec(memory_space=pl.ANY)] * 2,
         scratch_shapes=[
             pltpu.VMEM((block_cols, block_rows), jnp.float32),
-            pltpu.VMEM((block_cols, block_rows), jnp.bfloat16),
-            pltpu.VMEM((block_cols, block_rows), jnp.bfloat16),
+            pltpu.VMEM((3 * block_cols, block_rows), jnp.bfloat16),
             pltpu.VMEM((panel_cols, block_cols), jnp.bfloat16),
             pltpu.VMEM((panel_cols, block_cols), jnp.bfloat16),
-            pltpu.VMEM((panel_cols, block_cols), jnp.bfloat16),
-            pltpu.VMEM((panel_cols, block_cols), jnp.bfloat16),
+            pltpu.VMEM((panel_cols, 3 * block_cols), jnp.bfloat16),
             pltpu.VMEM((half_cols, block_rows), jnp.float32),
             pltpu.VMEM((half_cols, block_rows), jnp.float32),
             pltpu.SemaphoreType.DMA((vec_chunks,)),
@@ -390,7 +403,6 @@
         ],
         name="panel",
     )(
-        col_index[None],
         rotation_mate.reshape(-1, LANES),
         givens_theta.reshape(-1, LANES),
         kept_vectors[None, :],
@@ -402,7 +414,29 @@
     spot = spot[0]
     recv_rank = jnp.sum((same_owner & (mates[None, :] < mates[:, None])).astype(jnp.int32), axis=1)
     remote = owner != col_index
-    mate_row = jnp.where(remote, block_cols + owner * pair_cap + recv_rank, mates - first_col)
+    mate_row = jnp.where(remote, owner * pair_cap + recv_rank, 0)
+    far_sine = jnp.where(remote[None, :], sine, 0.0)
+    turned = pl.pallas_call(
+        turn_kernel,
+        out_shape=pltpu.VMEM((block_cols, lane_tiles, LANES), jnp.float32),
+        in_specs=[pl.BlockSpec(memory_space=pl.ANY)] * 4,
+        out_specs=pl.BlockSpec(memory_space=pltpu.VMEM),
+        scratch_shapes=[
+            pltpu.SMEM((1, block_cols), jnp.int32),
+            pltpu.SMEM((1, block_cols), jnp.float32),
+            pltpu.SMEM((1, block_cols), jnp.float32),
+            pltpu.VMEM(tiles.shape, jnp.float32),
+            pltpu.VMEM((block_cols, lane_tiles, LANES), jnp.float32),
+            pltpu.SemaphoreType.DMA((4,)),
+        ],
+        compiler_params=pltpu.CompilerParams(vmem_limit_bytes=40 * 1024 * 1024),
+        name="turn",
+    )(
+        jnp.where(remote, order, mates - first_col)[None, :],
+        cosine,
+        jnp.where(remote[None, :], 0.0, sine),
+        tiles,
+    )
     dest = spot // every
     dest_rank = jnp.sum(
         ((dest[:, None] == dest[None, :]) & (spot[None, :] < spot[:, None])).astype(jnp.int32),
@@ -415,22 +449,20 @@
     parcels = pl.pallas_call(
         functools.partial(pack_kernel, pieces),
         out_shape=jax.ShapeDtypeStruct((places, lane_tiles, LANES), jnp.float32),
-        in_specs=[pl.BlockSpec(memory_space=pl.ANY)] * 6,
+        in_specs=[pl.BlockSpec(memory_space=pl.ANY)] * 3
+        + [pl.BlockSpec(memory_space=pltpu.VMEM)] * 2,
         out_specs=pl.BlockSpec(memory_space=pl.ANY),
         scratch_shapes=[
             pltpu.SMEM((1, places), jnp.int32),
             pltpu.SMEM((1, block_cols), jnp.int32),
             pltpu.SMEM((1, block_cols), jnp.float32),
-            pltpu.SMEM((1, block_cols), jnp.float32),
-            pltpu.VMEM(tiles.shape, jnp.float32),
-            pltpu.VMEM((block_cols + slot_count, lane_tiles, LANES), jnp.float32),
             pltpu.VMEM((places, lane_tiles, LANES), jnp.float32),
-            pltpu.SemaphoreType.DMA((6,)),
+            pltpu.SemaphoreType.DMA((3,)),
             pltpu.SemaphoreType.DMA((pieces,)),
         ],
-        compiler_params=pltpu.CompilerParams(vmem_limit_bytes=50 * 1024 * 1024),
+        compiler_params=pltpu.CompilerParams(vmem_limit_bytes=48 * 1024 * 1024),
         name="rotate_pack",
-    )(place_source[None, :], mate_row[None, :], cosine, sine, tiles, incoming)
+    )(place_source[None, :], mate_row[None, :], far_sine, turned, incoming)
     arrived = lax.all_to_all(
         parcels.reshape(dest_count, move_cap * lane_tiles, LANES),
         ("row", "col"), split_axis=0, concat_axis=0, tiled=True,
@@ -461,6 +493,11 @@
     down = shift(jnp.concatenate([pair(2, high), pair(3, low)]), -1)
     up_low = shift(pair(1, low) + up[:half], 1)
     down_high = shift(pair(3, high) + down[:half], -1)
+
+    base = pair(0, slice(0, share)) + jnp.concatenate([down[half:], up[half:]])
+    base = lax.optimization_barrier(base * scale[:, None])
+    panel = base + jnp.concatenate([up_low, down_high]) * scale[:, None]
+    arrived, panel = lax.optimization_barrier((arrived, panel))
 
     slot_index = lax.axis_index("row") * col_count + col_index
     wanted = lax.dynamic_slice_in_dim(kept_vectors, slot_index * every, every)
@@ -491,10 +528,6 @@
         name="unpack",
     )(starts[None, :], arrived.reshape(row_count, col_count * move_cap, lane_tiles, LANES))
     packed_vectors = from_tiles(packed.reshape(-1, LANES), every, row_count * block_rows)
-    base = pair(0, slice(0, share)) + jnp.concatenate([down[half:], up[half:]])
-    base = lax.optimization_barrier(base * scale[:, None])
-    packed_vectors, up_low, down_high = lax.optimization_barrier((packed_vectors, up_low, down_high))
-    panel = base + jnp.concatenate([up_low, down_high]) * scale[:, None]
     return (packed_vectors, panel)
 
 

time: 118 us -> 120 us (1.017)
  local copies, waits for them, and re-layouts: 2.11 us -> 5.01 us
    unnamed x10 -> x16, local copies, waits for them, and re-layouts: 1.35 us -> 4.25 us
    all_to_all x1, waiting for transfers between devices: 9.22 us -> 6.83 us  [shards(): lax.all_to_all(outgoing, 'col', split_axis=0, concat_axis=0, tiled=True)]
    pallas_call x0 -> x1, Pallas kernels: none -> 1.7 us  [shards(): pl.pallas_call(turn_kernel, out_shape=pltpu.VMEM((block_cols, lane_tiles,...]
    ppermute x4, waiting for transfers between devices: 53.2 us -> 54.9 us  [shift(): return lax.ppermute(array, 'col', pairs)]
    pallas_call x1, Pallas kernels: 9 us -> 7.42 us  [shards(): pl.pallas_call(panel_kernel, out_shape=[jax.ShapeDtypeStruct((1, block_co...]
    ppermute x4, starting transfers between devices: 4.35 us -> 5.55 us  [shift(): return lax.ppermute(array, 'col', pairs)]
  transfers between devices with their start and end apart: 7 -> 7, of which waited for: 4 -> 3; matrix products, arithmetic and copies ran while one was open for 8% -> 9% of each run, Pallas kernels for 15% -> 11%
where the time goes in v4:
time: 120 us; the launch traced here: 119 us
  waiting for transfers between devices  61.7 us (51%)
  starting transfers between devices  21 us (18%)
  Pallas kernels  20.8 us (17%)
  other arithmetic  9.52 us (8%)
  local copies, waits for them, and re-layouts  5.01 us (4%)
    ppermute x4, waiting for transfers between devices, shift(): return lax.ppermute(array, 'col', pairs)  54.9 us
    all_to_all x1, starting transfers between devices, shards(): lax.all_to_all(parcels.reshape(dest_count, move_cap * lane_tiles, LANES),...  9.57 us
    pallas_call x1, Pallas kernels, shards(): pl.pallas_call(panel_kernel, out_shape=[jax.ShapeDtypeStruct((1, block_co...  7.42 us
    all_to_all x1, waiting for transfers between devices, shards(): lax.all_to_all(outgoing, 'col', split_axis=0, concat_axis=0, tiled=True)  6.83 us
    all_to_all x1, starting transfers between devices, shards(): lax.all_to_all(outgoing, 'col', split_axis=0, concat_axis=0, tiled=True)  5.8 us
    ppermute x4, starting transfers between devices, shift(): return lax.ppermute(array, 'col', pairs)  5.55 us
    pallas_call x1, Pallas kernels, shards(): pl.pallas_call(functools.partial(pack_kernel, pieces), out_shape=jax.Shap...  4.37 us
    unnamed x16, local copies, waits for them, and re-layouts  4.25 us
  transfers between devices with their start and end apart: 7, of which 3 were waited for; matrix products, arithmetic and copies ran while one was open for 9% of the time, Pallas kernels for 11%

profile of v4, /device:TPU:1, one launch (start us, length us, event | category | flops | bytes accessed | tf_op | source)
XLA Modules:
  0.0 118.9 jit_solution(798127053421031707)
XLA Ops:
  0.6 4.0 %send.1 = f32[192,16,128]{2,1,0:T(8,128)} custom-call(s32[24,128]{1,0:T(8,128)} %bitcast.46, f32[48,128,128]{2,1,0:T(8,128)} %bitcast.39), custom_call_target="tpu_custom_call" | custom-call | tf_op jit(solution)/shard_map/send/pallas_call | solution.py:361
  4.7 5.8 %all-to-all-start = ((f32[192,16,128]{2,1,0:T(8,128)}), f32[192,16,128]{2,1,0:T(8,128)}, u32[]{:S(2)}, u32[]{:S(2)}) async-start(f32[192,16,128]{2,1,0:T(8,128)} %send.1), calls=%async_computation | async-start | bytes 3145728 | tf_op jit(solution)/shard_map/all_to_all | solution.py:376
  10.5 0.0 copy-start
  10.5 7.4 %panel.1 = (s32[1,384]{1,0:T(1,128)}, f32[1,384]{1,0:T(1,128)}, f32[1,384]{1,0:T(1,128)}, f32[256,2048]{1,0:T(8,128)}, f32[256,2048]{1,0:T(8,128)}) custom-call(s32[24,128]{1,0:T(8,128)} %bitcast.47, f32[24,128]{1,0:T(8,128)} %bitcast.51, s32[1,3072]{1,0:T(1,128)} %bitcast.50, f32[1,3072]{1,0:T(1,128)} %bitcast.48, f32[1,3072]{1,0:T(1,128)} %bitcast.49, ...), custom_call_target="tpu_custom_call" | custom-call | tf_op jit(solution)/shard_map/panel/pallas_call | solution.py:380
  17.9 0.1 collective-permute-start
  18.0 0.8 subtract_select_fusion
  18.8 0.3 convert_reduce_fusion
  19.0 0.7 reshape_select_fusion
  19.7 0.0 copy-done
  19.8 0.0 copy-start.3
  19.8 0.7 copy-done.3
  20.4 0.0 copy-start.7
  20.4 1.7 %turn.1.turned_ref = f32[384,16,128]{2,1,0:T(8,128)S(1)} custom-call(s32[1,384]{1,0:T(1,128)S(1)} %broadcast_in_dim.73.mate_hbm, f32[1,384]{1,0:T(1,128)S(1)} %copy-done.3, f32[1,384]{1,0:T(1,128)S(1)} %get-tuple-element.30.sin_hbm, f32[48,128,128]{2,1,0:T(8,128)S(1)} %bitcast.40), custom_call_target="tpu_custom_call" | custom-call | tf_op jit(solution)/shard_map/turn/pallas_call | solution.py:419
  22.1 0.0 copy-start.1
  22.2 1.7 %copy-done.1 = f32[384,16,128]{2,1,0:T(8,128)} copy-done((f32[384,16,128]{2,1,0:T(8,128)}, f32[384,16,128]{2,1,0:T(8,128)S(1)}, u32[]{:S(2)}) %copy-start.1) | copy-done | bytes 3145752
  23.8 0.0 copy-done.7
  23.9 0.3 convert_reduce_fusion.1
  24.2 0.2 select_reduce_fusion
  24.3 6.8 %all-to-all-done.mates_ref = f32[192,16,128]{2,1,0:T(8,128)} async-done(((f32[192,16,128]{2,1,0:T(8,128)}), f32[192,16,128]{2,1,0:T(8,128)}, u32[]{:S(2)}, u32[]{:S(2)}) %all-to-all-start) | async-done | bytes 1572896 | tf_op jit(solution)/shard_map/all_to_all | solution.py:376
  31.1 1.9 %copy-done.2 = f32[384,16,128]{2,1,0:T(8,128)S(1)} copy-done((f32[384,16,128]{2,1,0:T(8,128)S(1)}, f32[384,16,128]{2,1,0:T(8,128)}, u32[]{:S(2)}) %copy-start.2) | copy-done | bytes 3145752
  33.0 4.4 %rotate_pack.1 = f32[512,16,128]{2,1,0:T(8,128)} custom-call(s32[1,512]{1,0:T(1,128)S(1)} %bitcast.41, s32[1,384]{1,0:T(1,128)S(1)} %broadcast_in_dim.70.mate_hbm, f32[1,384]{1,0:T(1,128)S(1)} %get-tuple-element.31.sin_hbm, f32[384,16,128]{2,1,0:T(8,128)S(1)} %copy-done.2, f32[192,16,128]{2,1,0:T(8,128)} %all-to-all-done.mates_ref), custom_call_target="tpu_custom_call" | custom-call | tf_op jit(solution)/shard_map/rotate_pack/pallas_call | solution.py:449
  37.4 0.0 copy-start.5
  37.4 0.0 copy-start.6
  37.4 0.0 copy-start.4
  37.5 9.6 %all-to-all-start.1 = ((f32[128,64,128]{2,1,0:T(8,128)}), f32[128,64,128]{2,1,0:T(8,128)}, u32[]{:S(2)}, u32[]{:S(2)}) async-start(f32[128,64,128]{2,1,0:T(8,128)} %bitcast.42), calls=%async_computation.1 | async-start | bytes 8388608 | tf_op jit(solution)/shard_map/all_to_all | solution.py:466
  47.0 0.8 dynamic_slice.11
  47.8 0.8 and_select_fusion.1
  48.6 0.0 copy-done.5
  48.6 0.0 copy-done.6
  48.6 0.3 multiply_reduce_fusion
  48.9 0.0 collective-permute-done
  48.9 0.0 copy-done.4
  48.9 1.3 %fusion.8 = (f32[32,2048]{1,0:T(8,128)S(1)}, f32[32,2048]{1,0:T(8,128)S(1)}, f32[32,2048]{1,0:T(8,128)S(1)}, f32[32,2048]{1,0:T(8,128)S(1)}) fusion(f32[4,64,2048]{2,1,0:T(8,128)} %bitcast.15, f32[4,64,2048]{2,1,0:T(8,128)S(1)} %bitcast.44), kind=kLoop, calls=%fused_computation.25 | loop fusion | flops 262144 | bytes 3145728 | tf_op jit(solution)/shard_map/add | solution.py:489
  50.3 1.4 %collective-permute-start.2 = (f32[64,2048]{1,0:T(8,128)S(1)}, f32[64,2048]{1,0:T(8,128)S(1)}, u32[]{:S(2)}, u32[]{:S(2)}) collective-permute-start(f32[64,2048]{1,0:T(8,128)S(1)} %pad_maximum_fusion.1), channel_id=1, source_target_pairs={{0,2},{1,3},{2,4},{3,5},{4,6},{5,7},{6,0},{7,1},{8,10},{9,11},{10,... | collective-permute-start | bytes 1572872 | tf_op jit(solution)/shard_map/ppermute | solution.py:480
  51.7 1.4 %collective-permute-start.1 = (f32[64,2048]{1,0:T(8,128)S(1)}, f32[64,2048]{1,0:T(8,128)S(1)}, u32[]{:S(2)}, u32[]{:S(2)}) collective-permute-start(f32[64,2048]{1,0:T(8,128)S(1)} %pad_maximum_fusion), channel_id=1, source_target_pairs={{0,6},{1,7},{2,0},{3,1},{4,2},{5,3},{6,4},{7,5},{8,14},{9,15},{10,... | collective-permute-start | bytes 1572872 | tf_op jit(solution)/shard_map/ppermute | solution.py:480
  53.1 0.2 convert_reduce_fusion.2
  53.3 1.4 %add_bitcast_fusion.start_hbm = s32[1,24]{1,0:T(1,128)} fusion(s32[24]{0:T(128)S(1)} %convert_reduce_fusion.2, s32[3072]{0:T(1024)} %param.10, s32[]{:T(128)S(6)} %select_n.49), kind=kLoop, calls=%fused_computation.46 | loop fusion | flops 240 | bytes 292 | tf_op jit(solution)/shard_map/broadcast_in_dim | solution.py:529
  54.7 50.6 %collective-permute-done.2 = f32[64,2048]{1,0:T(8,128)S(1)} collective-permute-done((f32[64,2048]{1,0:T(8,128)S(1)}, f32[64,2048]{1,0:T(8,128)S(1)}, u32[]{:S(2)}, u32[]{:S(2)}) %collective-permute-start.2) | collective-permute-done | bytes 524320 | tf_op jit(solution)/shard_map/ppermute | solution.py:480
  105.3 0.0 collective-permute-done.1
  105.3 1.2 slice_add_fusion.3
  106.5 0.1 collective-permute-start.3
  106.6 2.7 %collective-permute-start.4 = (f32[32,2048]{1,0:T(8,128)S(1)}, f32[32,2048]{1,0:T(8,128)S(1)}, u32[]{:S(2)}, u32[]{:S(2)}) collective-permute-start(f32[32,2048]{1,0:T(8,128)S(1)} %get-tuple-element.23), channel_id=1, source_target_pairs={{0,6},{1,7},{2,0},{3,1},{4,2},{5,3},{6,4},{7,5},{8,14},{9,15},{10,... | collective-permute-start | bytes 786440 | tf_op jit(solution)/shard_map/ppermute | solution.py:480
  109.2 1.2 fusion.1
  110.4 4.2 %collective-permute-done.3 = f32[32,2048]{1,0:T(8,128)S(1)} collective-permute-done((f32[32,2048]{1,0:T(8,128)S(1)}, f32[32,2048]{1,0:T(8,128)S(1)}, u32[]{:S(2)}, u32[]{:S(2)}) %collective-permute-start.3) | collective-permute-done | bytes 262176 | tf_op jit(solution)/shard_map/ppermute | solution.py:480
  114.7 0.0 collective-permute-done.4
  114.7 0.9 fusion.2
  115.6 0.0 all-to-all-done.1
  115.6 3.3 %unpack.1 = f32[3,16,128,128]{3,2,1,0:T(8,128)} custom-call(s32[1,24]{1,0:T(1,128)} %add_bitcast_fusion.start_hbm, f32[16,32,16,128]{3,2,1,0:T(8,128)} %bitcast.22.in_hbm), custom_call_target="tpu_custom_call" | custom-call | tf_op jit(solution)/shard_map/unpack/pallas_call | solution.py:513
  (10 shorter events, 0.2 us)
Async XLA Ops:
  4.7 26.5 %all-to-all-start = ((f32[192,16,128]{2,1,0:T(8,128)}), f32[192,16,128]{2,1,0:T(8,128)}, u32[]{:S(2)}, u32[]{:S(2)}) async-start(f32[192,16,128]{2,1,0:T(8,128)} %send.1), calls=%async_computation | async-start | bytes 3145728 | tf_op jit(solution)/shard_map/all_to_all | solution.py:376
  10.5 9.3 %copy-start = (f32[384,2048]{1,0:T(8,128)S(1)}, f32[384,2048]{1,0:T(8,128)}, u32[]{:S(2)}) copy-start(f32[384,2048]{1,0:T(8,128)} %vec_hbm.1) | copy-start | bytes 9437188
  17.9 31.0 %collective-permute-start = (f32[256,2048]{1,0:T(8,128)}, f32[256,2048]{1,0:T(8,128)}, u32[]{:S(2)}, u32[]{:S(2)}) collective-permute-start(f32[256,2048]{1,0:T(8,128)} %get-tuple-element.13), channel_id=1, source_target_pairs={{0,1},{1,0},{2,3},{3,2},{4,5},{5,4},{6,7},{7,6},{8,9},{9,8},{10,11... | collective-permute-start | bytes 6291464 | tf_op jit(solution)/shard_map/ppermute | solution.py:483
  19.8 0.7 copy-start.3
  20.4 3.4 %copy-start.7 = (s32[1,384]{1,0:T(1,128)S(1)}, s32[1,384]{1,0:T(1,128)}, u32[]{:S(2)}) copy-start(s32[1,384]{1,0:T(1,128)} %get-tuple-element.9) | copy-start | bytes 4612
  22.1 1.7 %copy-start.1 = (f32[384,16,128]{2,1,0:T(8,128)}, f32[384,16,128]{2,1,0:T(8,128)S(1)}, u32[]{:S(2)}) copy-start(f32[384,16,128]{2,1,0:T(8,128)S(1)} %turn.1.turned_ref) | copy-start | bytes 9437188
  31.1 1.9 %copy-start.2 = (f32[384,16,128]{2,1,0:T(8,128)S(1)}, f32[384,16,128]{2,1,0:T(8,128)}, u32[]{:S(2)}) copy-start(f32[384,16,128]{2,1,0:T(8,128)} %copy-done.1) | copy-start | bytes 9437188
  37.4 11.2 %copy-start.5 = (f32[3072]{0:T(1024)S(1)}, f32[3072]{0:T(1024)}, u32[]{:S(2)}) copy-start(f32[3072]{0:T(1024)} %param.11) | copy-start | bytes 36868
  37.4 11.2 %copy-start.6 = (f32[3072]{0:T(1024)S(1)}, f32[3072]{0:T(1024)}, u32[]{:S(2)}) copy-start(f32[3072]{0:T(1024)} %param.12) | copy-start | bytes 36868
  37.4 11.5 %copy-start.4 = (f32[256,2048]{1,0:T(8,128)S(1)}, f32[256,2048]{1,0:T(8,128)}, u32[]{:S(2)}) copy-start(f32[256,2048]{1,0:T(8,128)} %get-tuple-element.12) | copy-start | bytes 6291460
  37.5 78.2 %all-to-all-start.1 = ((f32[128,64,128]{2,1,0:T(8,128)}), f32[128,64,128]{2,1,0:T(8,128)}, u32[]{:S(2)}, u32[]{:S(2)}) async-start(f32[128,64,128]{2,1,0:T(8,128)} %bitcast.42), calls=%async_computation.1 | async-start | bytes 8388608 | tf_op jit(solution)/shard_map/all_to_all | solution.py:466
  50.3 55.0 %collective-permute-start.2 = (f32[64,2048]{1,0:T(8,128)S(1)}, f32[64,2048]{1,0:T(8,128)S(1)}, u32[]{:S(2)}, u32[]{:S(2)}) collective-permute-start(f32[64,2048]{1,0:T(8,128)S(1)} %pad_maximum_fusion.1), channel_id=1, source_target_pairs={{0,2},{1,3},{2,4},{3,5},{4,6},{5,7},{6,0},{7,1},{8,10},{9,11},{10,... | collective-permute-start | bytes 1572872 | tf_op jit(solution)/shard_map/ppermute | solution.py:480
  51.7 53.6 %collective-permute-start.1 = (f32[64,2048]{1,0:T(8,128)S(1)}, f32[64,2048]{1,0:T(8,128)S(1)}, u32[]{:S(2)}, u32[]{:S(2)}) collective-permute-start(f32[64,2048]{1,0:T(8,128)S(1)} %pad_maximum_fusion), channel_id=1, source_target_pairs={{0,6},{1,7},{2,0},{3,1},{4,2},{5,3},{6,4},{7,5},{8,14},{9,15},{10,... | collective-permute-start | bytes 1572872 | tf_op jit(solution)/shard_map/ppermute | solution.py:480
  106.5 8.2 %collective-permute-start.3 = (f32[32,2048]{1,0:T(8,128)S(1)}, f32[32,2048]{1,0:T(8,128)S(1)}, u32[]{:S(2)}, u32[]{:S(2)}) collective-permute-start(f32[32,2048]{1,0:T(8,128)S(1)} %get-tuple-element.22), channel_id=1, source_target_pairs={{0,2},{1,3},{2,4},{3,5},{4,6},{5,7},{6,0},{7,1},{8,10},{9,11},{10,... | collective-permute-start | bytes 786440 | tf_op jit(solution)/shard_map/ppermute | solution.py:480
  106.6 8.1 %collective-permute-start.4 = (f32[32,2048]{1,0:T(8,128)S(1)}, f32[32,2048]{1,0:T(8,128)S(1)}, u32[]{:S(2)}, u32[]{:S(2)}) collective-permute-start(f32[32,2048]{1,0:T(8,128)S(1)} %get-tuple-element.23), channel_id=1, source_target_pairs={{0,6},{1,7},{2,0},{3,1},{4,2},{5,3},{6,4},{7,5},{8,14},{9,15},{10,... | collective-permute-start | bytes 786440 | tf_op jit(solution)/shard_map/ppermute | solution.py:480

commit v5 on v4

--- a/solution.py
+++ b/solution.py
@@ -257,12 +257,15 @@
     lax.fori_loop(0, rows_ref.shape[0] // GROUP, turn, 0, unroll=2)
 
 
-def pack_kernel(pieces, source_hbm, mate_hbm, sin_hbm, turned_ref, mates_ref, out_hbm,
-                source_ref, mate_ref, sin_ref, stage_ref, load_sems, store_sems):
+def pack_kernel(pieces, source_hbm, mate_hbm, sin_hbm, turned_ref, mates_hbm, out_hbm,
+                source_ref, mate_ref, sin_ref, mates_ref, stage_ref, load_sems, store_sems):
     tables = [
         pltpu.make_async_copy(table, ref, load_sems.at[n])
         for n, (table, ref) in enumerate(
-            ((source_hbm, source_ref), (mate_hbm, mate_ref), (sin_hbm, sin_ref))
+            (
+                (mates_hbm, mates_ref), (source_hbm, source_ref),
+                (mate_hbm, mate_ref), (sin_hbm, sin_ref),
+            )
         )
     ]
     for table in tables:
@@ -359,7 +362,7 @@
     slot_count = col_count * pair_cap
     pieces = 4
     outgoing = pl.pallas_call(
-        functools.partial(send_kernel, pair_cap, pieces),
+        functools.partial(send_kernel, pair_cap, 2 * pieces),
         out_shape=jax.ShapeDtypeStruct((slot_count, lane_tiles, LANES), jnp.float32),
         in_specs=[pl.BlockSpec(memory_space=pl.ANY)] * 2,
         out_specs=pl.BlockSpec(memory_space=pl.ANY),
@@ -369,7 +372,7 @@
             pltpu.VMEM((slot_count, lane_tiles, LANES), jnp.float32),
             pltpu.VMEM((1, slot_count), jnp.int32),
             pltpu.SMEM((1, slot_count), jnp.int32),
-            pltpu.SemaphoreType.DMA((2 + pieces,)),
+            pltpu.SemaphoreType.DMA((2 + 2 * pieces,)),
         ],
         name="send",
     )(rotation_mate.reshape(-1, LANES), tiles)
@@ -447,18 +450,19 @@
     filled = dest_slot[None, :] == jnp.arange(places, dtype=jnp.int32)[:, None]
     place_source = one_hot_sum(filled, order)
     parcels = pl.pallas_call(
-        functools.partial(pack_kernel, pieces),
+        functools.partial(pack_kernel, 2 * pieces),
         out_shape=jax.ShapeDtypeStruct((places, lane_tiles, LANES), jnp.float32),
         in_specs=[pl.BlockSpec(memory_space=pl.ANY)] * 3
-        + [pl.BlockSpec(memory_space=pltpu.VMEM)] * 2,
+        + [pl.BlockSpec(memory_space=pltpu.VMEM), pl.BlockSpec(memory_space=pl.ANY)],
         out_specs=pl.BlockSpec(memory_space=pl.ANY),
         scratch_shapes=[
             pltpu.SMEM((1, places), jnp.int32),
             pltpu.SMEM((1, block_cols), jnp.int32),
             pltpu.SMEM((1, block_cols), jnp.float32),
+            pltpu.VMEM((slot_count, lane_tiles, LANES), jnp.float32),
             pltpu.VMEM((places, lane_tiles, LANES), jnp.float32),
-            pltpu.SemaphoreType.DMA((3,)),
-            pltpu.SemaphoreType.DMA((pieces,)),
+            pltpu.SemaphoreType.DMA((4,)),
+            pltpu.SemaphoreType.DMA((2 * pieces,)),
         ],
         compiler_params=pltpu.CompilerParams(vmem_limit_bytes=48 * 1024 * 1024),
         name="rotate_pack",

time: 120 us -> 119 us (level)
  no operation moved by 1% of the time
where the time goes in v5:
time: 119 us; the launch traced here: 118 us
  waiting for transfers between devices  61.7 us (52%)
  starting transfers between devices  21 us (18%)
  Pallas kernels  20 us (17%)
  other arithmetic  9.52 us (8%)
  local copies, waits for them, and re-layouts  5.01 us (4%)
    ppermute x4, waiting for transfers between devices, shift(): return lax.ppermute(array, 'col', pairs)  54.9 us
    all_to_all x1, starting transfers between devices, shards(): lax.all_to_all(parcels.reshape(dest_count, move_cap * lane_tiles, LANES),...  9.57 us
    pallas_call x1, Pallas kernels, shards(): pl.pallas_call(panel_kernel, out_shape=[jax.ShapeDtypeStruct((1, block_co...  7.42 us
    all_to_all x1, waiting for transfers between devices, shards(): lax.all_to_all(outgoing, 'col', split_axis=0, concat_axis=0, tiled=True)  6.83 us
    all_to_all x1, starting transfers between devices, shards(): lax.all_to_all(outgoing, 'col', split_axis=0, concat_axis=0, tiled=True)  5.8 us
    ppermute x4, starting transfers between devices, shift(): return lax.ppermute(array, 'col', pairs)  5.55 us
    unnamed x16, local copies, waits for them, and re-layouts  4.25 us
    pallas_call x1, Pallas kernels, shards(): pl.pallas_call(functools.partial(send_kernel, pair_cap, 2 * pieces), out_...  3.87 us
  transfers between devices with their start and end apart: 7, of which 3 were waited for; matrix products, arithmetic and copies ran while one was open for 9% of the time, Pallas kernels for 11%

profile of v5, /device:TPU:1, one launch (start us, length us, event | category | flops | bytes accessed | tf_op | source)
XLA Modules:
  0.0 118.1 jit_solution(17916335004132896220)
XLA Ops:
  0.6 3.9 %send.1 = f32[192,16,128]{2,1,0:T(8,128)} custom-call(s32[24,128]{1,0:T(8,128)} %bitcast.46, f32[48,128,128]{2,1,0:T(8,128)} %bitcast.39), custom_call_target="tpu_custom_call" | custom-call | tf_op jit(solution)/shard_map/send/pallas_call | solution.py:364
  4.5 5.8 %all-to-all-start = ((f32[192,16,128]{2,1,0:T(8,128)}), f32[192,16,128]{2,1,0:T(8,128)}, u32[]{:S(2)}, u32[]{:S(2)}) async-start(f32[192,16,128]{2,1,0:T(8,128)} %send.1), calls=%async_computation | async-start | bytes 3145728 | tf_op jit(solution)/shard_map/all_to_all | solution.py:379
  10.3 0.0 copy-start
  10.3 7.4 %panel.1 = (s32[1,384]{1,0:T(1,128)}, f32[1,384]{1,0:T(1,128)}, f32[1,384]{1,0:T(1,128)}, f32[256,2048]{1,0:T(8,128)}, f32[256,2048]{1,0:T(8,128)}) custom-call(s32[24,128]{1,0:T(8,128)} %bitcast.47, f32[24,128]{1,0:T(8,128)} %bitcast.51, s32[1,3072]{1,0:T(1,128)} %bitcast.50, f32[1,3072]{1,0:T(1,128)} %bitcast.48, f32[1,3072]{1,0:T(1,128)} %bitcast.49, ...), custom_call_target="tpu_custom_call" | custom-call | tf_op jit(solution)/shard_map/panel/pallas_call | solution.py:383
  17.7 0.1 collective-permute-start
  17.8 0.8 subtract_select_fusion
  18.6 0.3 convert_reduce_fusion
  18.9 0.7 reshape_select_fusion
  19.6 0.0 copy-done
  19.6 0.0 copy-start.3
  19.6 0.7 copy-done.3
  20.3 0.0 copy-start.7
  20.3 1.7 %turn.1.turned_ref = f32[384,16,128]{2,1,0:T(8,128)S(1)} custom-call(s32[1,384]{1,0:T(1,128)S(1)} %broadcast_in_dim.73.mate_hbm, f32[1,384]{1,0:T(1,128)S(1)} %copy-done.3, f32[1,384]{1,0:T(1,128)S(1)} %get-tuple-element.30.sin_hbm, f32[48,128,128]{2,1,0:T(8,128)S(1)} %bitcast.40), custom_call_target="tpu_custom_call" | custom-call | tf_op jit(solution)/shard_map/turn/pallas_call | solution.py:422
  22.0 0.0 copy-start.1
  22.0 1.7 %copy-done.1 = f32[384,16,128]{2,1,0:T(8,128)} copy-done((f32[384,16,128]{2,1,0:T(8,128)}, f32[384,16,128]{2,1,0:T(8,128)S(1)}, u32[]{:S(2)}) %copy-start.1) | copy-done | bytes 3145752
  23.7 0.0 copy-done.7
  23.7 0.3 convert_reduce_fusion.1
  24.0 0.2 select_reduce_fusion
  24.2 6.8 %all-to-all-done.mates_hbm = f32[192,16,128]{2,1,0:T(8,128)} async-done(((f32[192,16,128]{2,1,0:T(8,128)}), f32[192,16,128]{2,1,0:T(8,128)}, u32[]{:S(2)}, u32[]{:S(2)}) %all-to-all-start) | async-done | bytes 1572896 | tf_op jit(solution)/shard_map/all_to_all | solution.py:379
  31.0 1.9 %copy-done.2 = f32[384,16,128]{2,1,0:T(8,128)S(1)} copy-done((f32[384,16,128]{2,1,0:T(8,128)S(1)}, f32[384,16,128]{2,1,0:T(8,128)}, u32[]{:S(2)}) %copy-start.2) | copy-done | bytes 3145752
  32.9 3.7 %rotate_pack.1 = f32[512,16,128]{2,1,0:T(8,128)} custom-call(s32[1,512]{1,0:T(1,128)S(1)} %bitcast.41, s32[1,384]{1,0:T(1,128)S(1)} %broadcast_in_dim.70.mate_hbm, f32[1,384]{1,0:T(1,128)S(1)} %get-tuple-element.31.sin_hbm, f32[384,16,128]{2,1,0:T(8,128)S(1)} %copy-done.2, f32[192,16,128]{2,1,0:T(8,128)} %all-to-all-done.mates_hbm), custom_call_target="tpu_custom_call" | custom-call | tf_op jit(solution)/shard_map/rotate_pack/pallas_call | solution.py:452
  36.6 0.0 copy-start.5
  36.6 0.0 copy-start.6
  36.6 0.0 copy-start.4
  36.6 9.6 %all-to-all-start.1 = ((f32[128,64,128]{2,1,0:T(8,128)}), f32[128,64,128]{2,1,0:T(8,128)}, u32[]{:S(2)}, u32[]{:S(2)}) async-start(f32[128,64,128]{2,1,0:T(8,128)} %bitcast.42), calls=%async_computation.1 | async-start | bytes 8388608 | tf_op jit(solution)/shard_map/all_to_all | solution.py:470
  46.2 0.8 dynamic_slice.11
  47.0 0.8 and_select_fusion.1
  47.7 0.0 copy-done.5
  47.7 0.0 copy-done.6
  47.7 0.3 multiply_reduce_fusion
  48.1 0.0 collective-permute-done
  48.1 0.0 copy-done.4
  48.1 1.3 %fusion.8 = (f32[32,2048]{1,0:T(8,128)S(1)}, f32[32,2048]{1,0:T(8,128)S(1)}, f32[32,2048]{1,0:T(8,128)S(1)}, f32[32,2048]{1,0:T(8,128)S(1)}) fusion(f32[4,64,2048]{2,1,0:T(8,128)} %bitcast.15, f32[4,64,2048]{2,1,0:T(8,128)S(1)} %bitcast.44), kind=kLoop, calls=%fused_computation.25 | loop fusion | flops 262144 | bytes 3145728 | tf_op jit(solution)/shard_map/add | solution.py:493
  49.4 1.4 %collective-permute-start.2 = (f32[64,2048]{1,0:T(8,128)S(1)}, f32[64,2048]{1,0:T(8,128)S(1)}, u32[]{:S(2)}, u32[]{:S(2)}) collective-permute-start(f32[64,2048]{1,0:T(8,128)S(1)} %pad_maximum_fusion.1), channel_id=1, source_target_pairs={{0,2},{1,3},{2,4},{3,5},{4,6},{5,7},{6,0},{7,1},{8,10},{9,11},{10,... | collective-permute-start | bytes 1572872 | tf_op jit(solution)/shard_map/ppermute | solution.py:484
  50.9 1.4 %collective-permute-start.1 = (f32[64,2048]{1,0:T(8,128)S(1)}, f32[64,2048]{1,0:T(8,128)S(1)}, u32[]{:S(2)}, u32[]{:S(2)}) collective-permute-start(f32[64,2048]{1,0:T(8,128)S(1)} %pad_maximum_fusion), channel_id=1, source_target_pairs={{0,6},{1,7},{2,0},{3,1},{4,2},{5,3},{6,4},{7,5},{8,14},{9,15},{10,... | collective-permute-start | bytes 1572872 | tf_op jit(solution)/shard_map/ppermute | solution.py:484
  52.3 0.2 convert_reduce_fusion.2
  52.5 1.4 %add_bitcast_fusion.start_hbm = s32[1,24]{1,0:T(1,128)} fusion(s32[24]{0:T(128)S(1)} %convert_reduce_fusion.2, s32[3072]{0:T(1024)} %param.10, s32[]{:T(128)S(6)} %select_n.49), kind=kLoop, calls=%fused_computation.46 | loop fusion | flops 240 | bytes 292 | tf_op jit(solution)/shard_map/broadcast_in_dim | solution.py:533
  53.8 50.6 %collective-permute-done.2 = f32[64,2048]{1,0:T(8,128)S(1)} collective-permute-done((f32[64,2048]{1,0:T(8,128)S(1)}, f32[64,2048]{1,0:T(8,128)S(1)}, u32[]{:S(2)}, u32[]{:S(2)}) %collective-permute-start.2) | collective-permute-done | bytes 524320 | tf_op jit(solution)/shard_map/ppermute | solution.py:484
  104.5 0.0 collective-permute-done.1
  104.5 1.2 slice_add_fusion.3
  105.6 0.1 collective-permute-start.3
  105.7 2.7 %collective-permute-start.4 = (f32[32,2048]{1,0:T(8,128)S(1)}, f32[32,2048]{1,0:T(8,128)S(1)}, u32[]{:S(2)}, u32[]{:S(2)}) collective-permute-start(f32[32,2048]{1,0:T(8,128)S(1)} %get-tuple-element.23), channel_id=1, source_target_pairs={{0,6},{1,7},{2,0},{3,1},{4,2},{5,3},{6,4},{7,5},{8,14},{9,15},{10,... | collective-permute-start | bytes 786440 | tf_op jit(solution)/shard_map/ppermute | solution.py:484
  108.4 1.2 %fusion.1 = f32[64,2048]{1,0:T(8,128)S(1)} fusion(f32[256,2048]{1,0:T(8,128)} %collective-permute-done, f32[32,2048]{1,0:T(8,128)S(1)} %get-tuple-element.29, f32[32,2048]{1,0:T(8,128)S(1)} %get-tuple-element.28, f32[256,2048]{1,0:T(8,128)S(1)} %copy-done.4, f32[64]{0:T(128)S(1)} %add_rsqrt_fusion), kind=kLoop, calls=%fused_computation.7 | loop fusion | flops 524288 | bytes 2097408 | tf_op jit(solution)/shard_map/mul | solution.py:502
  109.6 4.2 %collective-permute-done.3 = f32[32,2048]{1,0:T(8,128)S(1)} collective-permute-done((f32[32,2048]{1,0:T(8,128)S(1)}, f32[32,2048]{1,0:T(8,128)S(1)}, u32[]{:S(2)}, u32[]{:S(2)}) %collective-permute-start.3) | collective-permute-done | bytes 262176 | tf_op jit(solution)/shard_map/ppermute | solution.py:484
  113.8 0.0 collective-permute-done.4
  113.8 0.9 fusion.2
  114.8 0.0 all-to-all-done.1
  114.8 3.3 %unpack.1 = f32[3,16,128,128]{3,2,1,0:T(8,128)} custom-call(s32[1,24]{1,0:T(1,128)} %add_bitcast_fusion.start_hbm, f32[16,32,16,128]{3,2,1,0:T(8,128)} %bitcast.22.in_hbm), custom_call_target="tpu_custom_call" | custom-call | tf_op jit(solution)/shard_map/unpack/pallas_call | solution.py:517
  (10 shorter events, 0.2 us)
Async XLA Ops:
  4.5 26.5 %all-to-all-start = ((f32[192,16,128]{2,1,0:T(8,128)}), f32[192,16,128]{2,1,0:T(8,128)}, u32[]{:S(2)}, u32[]{:S(2)}) async-start(f32[192,16,128]{2,1,0:T(8,128)} %send.1), calls=%async_computation | async-start | bytes 3145728 | tf_op jit(solution)/shard_map/all_to_all | solution.py:379
  10.3 9.3 %copy-start = (f32[384,2048]{1,0:T(8,128)S(1)}, f32[384,2048]{1,0:T(8,128)}, u32[]{:S(2)}) copy-start(f32[384,2048]{1,0:T(8,128)} %vec_hbm.1) | copy-start | bytes 9437188
  17.7 30.3 %collective-permute-start = (f32[256,2048]{1,0:T(8,128)}, f32[256,2048]{1,0:T(8,128)}, u32[]{:S(2)}, u32[]{:S(2)}) collective-permute-start(f32[256,2048]{1,0:T(8,128)} %get-tuple-element.13), channel_id=1, source_target_pairs={{0,1},{1,0},{2,3},{3,2},{4,5},{5,4},{6,7},{7,6},{8,9},{9,8},{10,11... | collective-permute-start | bytes 6291464 | tf_op jit(solution)/shard_map/ppermute | solution.py:487
  19.6 0.7 copy-start.3
  20.3 3.4 %copy-start.7 = (s32[1,384]{1,0:T(1,128)S(1)}, s32[1,384]{1,0:T(1,128)}, u32[]{:S(2)}) copy-start(s32[1,384]{1,0:T(1,128)} %get-tuple-element.9) | copy-start | bytes 4612
  22.0 1.7 %copy-start.1 = (f32[384,16,128]{2,1,0:T(8,128)}, f32[384,16,128]{2,1,0:T(8,128)S(1)}, u32[]{:S(2)}) copy-start(f32[384,16,128]{2,1,0:T(8,128)S(1)} %turn.1.turned_ref) | copy-start | bytes 9437188
  31.0 1.9 %copy-start.2 = (f32[384,16,128]{2,1,0:T(8,128)S(1)}, f32[384,16,128]{2,1,0:T(8,128)}, u32[]{:S(2)}) copy-start(f32[384,16,128]{2,1,0:T(8,128)} %copy-done.1) | copy-start | bytes 9437188
  36.6 11.2 %copy-start.5 = (f32[3072]{0:T(1024)S(1)}, f32[3072]{0:T(1024)}, u32[]{:S(2)}) copy-start(f32[3072]{0:T(1024)} %param.11) | copy-start | bytes 36868
  36.6 11.2 %copy-start.6 = (f32[3072]{0:T(1024)S(1)}, f32[3072]{0:T(1024)}, u32[]{:S(2)}) copy-start(f32[3072]{0:T(1024)} %param.12) | copy-start | bytes 36868
  36.6 11.5 %copy-start.4 = (f32[256,2048]{1,0:T(8,128)S(1)}, f32[256,2048]{1,0:T(8,128)}, u32[]{:S(2)}) copy-start(f32[256,2048]{1,0:T(8,128)} %get-tuple-element.12) | copy-start | bytes 6291460
  36.6 78.2 %all-to-all-start.1 = ((f32[128,64,128]{2,1,0:T(8,128)}), f32[128,64,128]{2,1,0:T(8,128)}, u32[]{:S(2)}, u32[]{:S(2)}) async-start(f32[128,64,128]{2,1,0:T(8,128)} %bitcast.42), calls=%async_computation.1 | async-start | bytes 8388608 | tf_op jit(solution)/shard_map/all_to_all | solution.py:470
  49.4 55.0 %collective-permute-start.2 = (f32[64,2048]{1,0:T(8,128)S(1)}, f32[64,2048]{1,0:T(8,128)S(1)}, u32[]{:S(2)}, u32[]{:S(2)}) collective-permute-start(f32[64,2048]{1,0:T(8,128)S(1)} %pad_maximum_fusion.1), channel_id=1, source_target_pairs={{0,2},{1,3},{2,4},{3,5},{4,6},{5,7},{6,0},{7,1},{8,10},{9,11},{10,... | collective-permute-start | bytes 1572872 | tf_op jit(solution)/shard_map/ppermute | solution.py:484
  50.9 53.6 %collective-permute-start.1 = (f32[64,2048]{1,0:T(8,128)S(1)}, f32[64,2048]{1,0:T(8,128)S(1)}, u32[]{:S(2)}, u32[]{:S(2)}) collective-permute-start(f32[64,2048]{1,0:T(8,128)S(1)} %pad_maximum_fusion), channel_id=1, source_target_pairs={{0,6},{1,7},{2,0},{3,1},{4,2},{5,3},{6,4},{7,5},{8,14},{9,15},{10,... | collective-permute-start | bytes 1572872 | tf_op jit(solution)/shard_map/ppermute | solution.py:484
  105.6 8.2 %collective-permute-start.3 = (f32[32,2048]{1,0:T(8,128)S(1)}, f32[32,2048]{1,0:T(8,128)S(1)}, u32[]{:S(2)}, u32[]{:S(2)}) collective-permute-start(f32[32,2048]{1,0:T(8,128)S(1)} %get-tuple-element.22), channel_id=1, source_target_pairs={{0,2},{1,3},{2,4},{3,5},{4,6},{5,7},{6,0},{7,1},{8,10},{9,11},{10,... | collective-permute-start | bytes 786440 | tf_op jit(solution)/shard_map/ppermute | solution.py:484
  105.7 8.1 %collective-permute-start.4 = (f32[32,2048]{1,0:T(8,128)S(1)}, f32[32,2048]{1,0:T(8,128)S(1)}, u32[]{:S(2)}, u32[]{:S(2)}) collective-permute-start(f32[32,2048]{1,0:T(8,128)S(1)} %get-tuple-element.23), channel_id=1, source_target_pairs={{0,6},{1,7},{2,0},{3,1},{4,2},{5,3},{6,4},{7,5},{8,14},{9,15},{10,... | collective-permute-start | bytes 786440 | tf_op jit(solution)/shard_map/ppermute | solution.py:484
